TPU v7x, 16 devices: a 4x2x1 block of a 4x4x8 slice. The times are simulated.
16 devices in a mesh: dp: 2 (over y, z), tp: 8 (over x, core).
Axes of the slice: x: 4, y: 2, z: 1, core: 2. Of those that a mesh axis runs over, the one named last changes fastest.
The devices are a block of a 4x4x8 slice.
Arguments:
- hidden: bfloat16 [6, 1024, 8192], P('dp', 'tp'), parts along dimension 0
- attn_gain: float32 [8192], replicated
- attn_bias: float32 [8192], replicated
- mlp_gain: float32 [8192], replicated
- mlp_bias: float32 [8192], replicated
- w_qkv: bfloat16 [8192, 8, 1152], P(None, 'tp')
- w_out: bfloat16 [8192, 8192], P('tp')
- w_up: bfloat16 [8192, 32768], P(None, 'tp')
- w_down: bfloat16 [32768, 8192], P('tp')
- positions: int32 [1024], replicated
Outputs:
- output: bfloat16 [6, 1024, 8192], P('dp', 'tp'), parts along dimension 0
There are 2 independent parts. A program takes and returns all parts, laid end to end along the dimension named above; an argument that names none is the same for every part.
All inputs are finite; a program needn't handle non-finite values.
Results may differ from a plain program's by a relative error of at most 0.00657861.
Values are sent between devices in bfloat16 or wider.
A program may use at most 768 MiB of HBM per device.

v0:
```python
import jax
import jax.numpy as jnp
from jax import lax
from jax.sharding import PartitionSpec as P


def layer_norm(tok_rows, norm_gain, norm_bias):
    rows32 = tok_rows.astype(jnp.float32)
    row_mean = jnp.mean(rows32, axis=-1, keepdims=True)
    centered = rows32 - row_mean
    row_var = jnp.mean(centered * centered, axis=-1, keepdims=True)
    return (centered * lax.rsqrt(row_var + 1e-5) * norm_gain + norm_bias).astype(jnp.bfloat16)


def rotary_tables(positions, head_dim):
    inv_freq = 10000.0 ** (-2.0 * jnp.arange(head_dim // 2, dtype=jnp.float32) / head_dim)
    angles = positions.astype(jnp.float32)[:, None] * inv_freq[None, :]
    angles = jnp.concatenate([angles, angles], axis=-1)
    return jnp.cos(angles), jnp.sin(angles)


def apply_rotary(head_vals, cos_tab, sin_tab):
    half_dim = head_vals.shape[-1] // 2
    vals32 = head_vals.astype(jnp.float32)
    rotated = jnp.concatenate([-vals32[..., half_dim:], vals32[..., :half_dim]], axis=-1)
    return (vals32 * cos_tab + rotated * sin_tab).astype(jnp.bfloat16)


def attention_branch(normed, w_qkv_part, w_out_part, positions):
    batch_size, seq_len, model_width = normed.shape
    num_groups = w_qkv_part.shape[1]
    slot_cols = w_qkv_part.shape[2]
    group_cols = w_out_part.shape[0] // num_groups
    head_dim = (slot_cols - group_cols) // 2
    group_size = group_cols // head_dim
    qkv_rows = jnp.einsum('bsd,dkc->bskc', normed, w_qkv_part, preferred_element_type=jnp.float32).astype(jnp.bfloat16)
    qkv_rows = qkv_rows.reshape(batch_size, seq_len, num_groups, group_size + 2, head_dim)
    cos_tab, sin_tab = rotary_tables(positions, head_dim)
    query_rot = apply_rotary(qkv_rows[:, :, :, :group_size, :], cos_tab[None, :, None, None, :], sin_tab[None, :, None, None, :])
    key_rot = apply_rotary(qkv_rows[:, :, :, group_size, :], cos_tab[None, :, None, :], sin_tab[None, :, None, :])
    value_seq = qkv_rows[:, :, :, group_size + 1, :]
    block_len = min(seq_len, 256)
    num_blocks = seq_len // block_len
    key_idx = jnp.arange(seq_len)
    score_scale = head_dim ** -0.5

    def one_block(block_idx):
        row_start = block_idx * block_len
        query_blk = lax.dynamic_slice_in_dim(query_rot, row_start, block_len, axis=1)
        scores = jnp.einsum('bqkgh,bskh->bkgqs', query_blk, key_rot, preferred_element_type=jnp.float32) * score_scale
        query_idx = row_start + jnp.arange(block_len)
        allowed = key_idx[None, :] <= query_idx[:, None]
        scores = jnp.where(allowed, scores, -1e30)
        exp_scores = jnp.exp(scores - jnp.max(scores, axis=-1, keepdims=True))
        attn_probs = (exp_scores / jnp.sum(exp_scores, axis=-1, keepdims=True)).astype(jnp.bfloat16)
        context = jnp.einsum('bkgqs,bskh->bqkgh', attn_probs, value_seq, preferred_element_type=jnp.float32)
        return context.astype(jnp.bfloat16).reshape(batch_size, block_len, num_groups * group_cols)

    ctx_blocks = lax.map(one_block, jnp.arange(num_blocks))
    attn_part = jnp.einsum('nbqc,cd->bnqd', ctx_blocks, w_out_part, preferred_element_type=jnp.float32)
    return attn_part.reshape(batch_size, seq_len, model_width)


def solution(mesh):
    def local_layer(hidden_blk, attn_gain, attn_bias, mlp_gain, mlp_bias, w_qkv_part, w_out_part, w_up_part, w_down_part, positions):
        normed_attn = layer_norm(hidden_blk, attn_gain, attn_bias)
        normed_mlp = layer_norm(hidden_blk, mlp_gain, mlp_bias)
        attn_in = lax.all_gather(normed_attn, 'tp', axis=1, tiled=True)
        mlp_in = lax.all_gather(normed_mlp, 'tp', axis=1, tiled=True)
        attn_part = attention_branch(attn_in, w_qkv_part, w_out_part, positions)
        up_pre = jnp.einsum('bsd,df->bsf', mlp_in, w_up_part, preferred_element_type=jnp.float32)
        up_act = jax.nn.gelu(up_pre, approximate=False).astype(jnp.bfloat16)
        mlp_part = jnp.einsum('bsf,fd->bsd', up_act, w_down_part, preferred_element_type=jnp.float32)
        token_sum = lax.psum_scatter(attn_part + mlp_part, 'tp', scatter_dimension=1, tiled=True)
        return (hidden_blk.astype(jnp.float32) + token_sum).astype(jnp.bfloat16)

    return jax.shard_map(local_layer, mesh=mesh, in_specs=(P('dp', 'tp', None), P(), P(), P(), P(), P(None, 'tp', None), P('tp', None), P(None, 'tp'), P('tp', None), P()), out_specs=P('dp', 'tp', None), check_vma=False)
```

profile of v0, /device:TPU:112, one launch (start us, length us, event | category | flops | bytes accessed | tf_op | source)
XLA Modules:
  0.0 1888.5 jit_solution(4769310236998898536)
XLA Ops:
  6.5 0.0 all-gather.3.cloned.1.call-start
  6.6 3.7 convert_reduce_fusion
  10.3 4.6 fusion.75
  14.8 9.2 fusion.74
  24.1 0.1 all-gather.3.cloned.1.call-update
  24.1 0.1 all-gather.5.cloned.1.call-start
  24.2 0.7 all-gather.5.cloned.1.call-update
  24.9 0.6 reduce-scatter.2.cloned.1.call-start
  25.5 0.7 convert_element_type.78
  26.2 0.1 broadcast_multiply_fusion
  26.3 1.0 fusion.90
  27.3 0.0 copy-start
  27.3 0.0 copy-start.1
  27.3 223.7 %all-gather.3.cloned.1.call-done = bf16[3,1024,8192]{2,1,0:T(8,128)(2,1)} async-done(((bf16[3,128,8192]{2,1,0:T(8,128)(2,1)}), bf16[3,1024,8192]{2,1,0:T(8,128)(2,1)}) %all-gather.3.cloned.1.call-update) | async-done | bytes 50331664 | tf_op jit(solution)/shard_map/all_gather | solution.py:68
  251.0 75.6 %fusion.81 = bf16[3,1024,1152]{2,1,0:T(8,128)(2,1)} fusion(bf16[3,1024,8192]{2,1,0:T(8,128)(2,1)} %all-gather.3.cloned.1.call-done, bf16[8192,1,1152]{2,0,1:T(8,128)(2,1)} %param.17), kind=kOutput, calls=%fused_computation.100 | convolution fusion | flops 57985597440 | bytes 76283904 | tf_op jit(solution)/shard_map/bsd,dkc->bskc/dot_general | solution.py:36
  326.7 10.5 copy.16
  337.1 2.0 slice_bitcast_fusion
  339.1 0.1 slice_negate_fusion.1
  339.2 0.0 copy-done
  339.2 0.0 copy-done.1
  339.2 1.2 fusion.87
  340.4 8.9 slice_convert_fusion
  349.3 9.4 slice_negate_fusion
  358.7 9.2 fusion.78
  367.9 257.7 %while.11 = (s32[]{:T(128)}, bf16[4,3,256,1024]{2,3,1,0:T(8,128)(2,1)}, s32[4]{0:T(128)S(1)}, bf16[3,1024,1,16,64]{1,4,3,0,2:T(8,128)(2,1)}, bf16[3,1024,1,64]{1...) while((s32[]{:T(128)}, ...), condition=%wide.region_5.6_spmd.clone, body=%wide.region_2.5_spmd.clone.sunk | while | flops 3373244672 | bytes 160942304 | solution.py:59
  367.9 0.6 dynamic_slice.18
  369.2 0.2 iota_compare_fusion.2
  369.4 0.0 copy-start.2
  369.4 20.0 %fusion.137 = (f32[3,16,256]{2,1,0:T(8,128)S(1)}, f32[3,256,16,1024]{3,1,2,0:T(8,128)}) fusion(pred[256,1024]{1,0:T(8,128)(4,1)S(1)} %iota_compare_fusion.2, bf16[3,1024,1,64]{1,3,0,2:T(8,128)(2,1)S(1)} %get-tuple-element.149, bf16[3,1024,1,16,64]{1,4,3,0,2:T(8,128)(2,1)} %get-tuple-element.148, s32[]{:T(128)S(6)} %select_n.28), kind=kOutput, calls=%fused_computation.5.clone.1 | convolution fusion | flops 1648349184 | bytes 52609028 | tf_op jit(solution)/shard_map/while/body/eval_jaxpr/bqkgh,bskh->bkgqs/dot_general | solution.py:50
  389.3 21.8 %fusion.138 = f32[3,16,256]{2,1,0:T(8,128)S(1)} fusion(f32[3,256,16,1024]{3,1,2,0:T(8,128)} %get-tuple-element.123, f32[3,16,256]{2,1,0:T(8,128)S(1)} %get-tuple-element.124, pred[256,1024]{1,0:T(8,128)(4,1)S(1)} %iota_compare_fusion.2), kind=kLoop, calls=%fused_computation.4.clone.1 | loop fusion | flops 50319360 | bytes 50692096 | tf_op jit(solution)/shard_map/while/body/eval_jaxpr/reduce_sum | solution.py:55
  411.1 0.0 copy-done.2
  411.1 20.0 %fusion.139 = bf16[3,16,256,64]{2,3,1,0:T(8,128)(2,1)S(1)} fusion(f32[3,16,256]{2,1,0:T(8,128)S(1)} %fusion.138, f32[3,16,256]{2,1,0:T(8,128)S(1)} %get-tuple-element.124, f32[3,256,16,1024]{3,1,2,0:T(8,128)} %get-tuple-element.123, pred[256,1024]{1,0:T(8,128)(4,1)S(1)} %iota_compare_fusion.2, bf16[3,1024,1,64]{1,3,0,2:T(8,128)(2,1)S(1)} %copy-done.2), kind=kOutput, calls=%fused_computation.8.clone.1 | convolution fusion | flops 1674313728 | bytes 52658176 | tf_op jit(solution)/shard_map/while/body/eval_jaxpr/bkgqs,bskh->bqkgh/dot_general | solution.py:56
  431.1 1.2 constant_dynamic-update-slice_fusion.2
  432.4 0.6 dynamic_slice.18
  433.6 0.2 iota_compare_fusion.2
  433.8 0.0 copy-start.2
  433.8 20.0 %fusion.137 = (f32[3,16,256]{2,1,0:T(8,128)S(1)}, f32[3,256,16,1024]{3,1,2,0:T(8,128)}) fusion(pred[256,1024]{1,0:T(8,128)(4,1)S(1)} %iota_compare_fusion.2, bf16[3,1024,1,64]{1,3,0,2:T(8,128)(2,1)S(1)} %get-tuple-element.149, bf16[3,1024,1,16,64]{1,4,3,0,2:T(8,128)(2,1)} %get-tuple-element.148, s32[]{:T(128)S(6)} %select_n.28), kind=kOutput, calls=%fused_computation.5.clone.1 | convolution fusion | flops 1648349184 | bytes 52609028 | tf_op jit(solution)/shard_map/while/body/eval_jaxpr/bqkgh,bskh->bkgqs/dot_general | solution.py:50
  453.8 21.8 %fusion.138 = f32[3,16,256]{2,1,0:T(8,128)S(1)} fusion(f32[3,256,16,1024]{3,1,2,0:T(8,128)} %get-tuple-element.123, f32[3,16,256]{2,1,0:T(8,128)S(1)} %get-tuple-element.124, pred[256,1024]{1,0:T(8,128)(4,1)S(1)} %iota_compare_fusion.2), kind=kLoop, calls=%fused_computation.4.clone.1 | loop fusion | flops 50319360 | bytes 50692096 | tf_op jit(solution)/shard_map/while/body/eval_jaxpr/reduce_sum | solution.py:55
  475.5 0.0 copy-done.2
  475.5 20.0 %fusion.139 = bf16[3,16,256,64]{2,3,1,0:T(8,128)(2,1)S(1)} fusion(f32[3,16,256]{2,1,0:T(8,128)S(1)} %fusion.138, f32[3,16,256]{2,1,0:T(8,128)S(1)} %get-tuple-element.124, f32[3,256,16,1024]{3,1,2,0:T(8,128)} %get-tuple-element.123, pred[256,1024]{1,0:T(8,128)(4,1)S(1)} %iota_compare_fusion.2, bf16[3,1024,1,64]{1,3,0,2:T(8,128)(2,1)S(1)} %copy-done.2), kind=kOutput, calls=%fused_computation.8.clone.1 | convolution fusion | flops 1674313728 | bytes 52658176 | tf_op jit(solution)/shard_map/while/body/eval_jaxpr/bkgqs,bskh->bqkgh/dot_general | solution.py:56
  495.5 1.2 constant_dynamic-update-slice_fusion.2
  496.8 0.6 dynamic_slice.18
  498.0 0.2 iota_compare_fusion.2
  498.2 0.0 copy-start.2
  498.2 20.0 %fusion.137 = (f32[3,16,256]{2,1,0:T(8,128)S(1)}, f32[3,256,16,1024]{3,1,2,0:T(8,128)}) fusion(pred[256,1024]{1,0:T(8,128)(4,1)S(1)} %iota_compare_fusion.2, bf16[3,1024,1,64]{1,3,0,2:T(8,128)(2,1)S(1)} %get-tuple-element.149, bf16[3,1024,1,16,64]{1,4,3,0,2:T(8,128)(2,1)} %get-tuple-element.148, s32[]{:T(128)S(6)} %select_n.28), kind=kOutput, calls=%fused_computation.5.clone.1 | convolution fusion | flops 1648349184 | bytes 52609028 | tf_op jit(solution)/shard_map/while/body/eval_jaxpr/bqkgh,bskh->bkgqs/dot_general | solution.py:50
  518.2 21.8 %fusion.138 = f32[3,16,256]{2,1,0:T(8,128)S(1)} fusion(f32[3,256,16,1024]{3,1,2,0:T(8,128)} %get-tuple-element.123, f32[3,16,256]{2,1,0:T(8,128)S(1)} %get-tuple-element.124, pred[256,1024]{1,0:T(8,128)(4,1)S(1)} %iota_compare_fusion.2), kind=kLoop, calls=%fused_computation.4.clone.1 | loop fusion | flops 50319360 | bytes 50692096 | tf_op jit(solution)/shard_map/while/body/eval_jaxpr/reduce_sum | solution.py:55
  540.0 0.0 copy-done.2
  540.0 20.0 %fusion.139 = bf16[3,16,256,64]{2,3,1,0:T(8,128)(2,1)S(1)} fusion(f32[3,16,256]{2,1,0:T(8,128)S(1)} %fusion.138, f32[3,16,256]{2,1,0:T(8,128)S(1)} %get-tuple-element.124, f32[3,256,16,1024]{3,1,2,0:T(8,128)} %get-tuple-element.123, pred[256,1024]{1,0:T(8,128)(4,1)S(1)} %iota_compare_fusion.2, bf16[3,1024,1,64]{1,3,0,2:T(8,128)(2,1)S(1)} %copy-done.2), kind=kOutput, calls=%fused_computation.8.clone.1 | convolution fusion | flops 1674313728 | bytes 52658176 | tf_op jit(solution)/shard_map/while/body/eval_jaxpr/bkgqs,bskh->bqkgh/dot_general | solution.py:56
  559.9 1.2 constant_dynamic-update-slice_fusion.2
  561.2 0.6 dynamic_slice.18
  562.4 0.2 iota_compare_fusion.2
  562.7 0.0 copy-start.2
  562.7 20.0 %fusion.137 = (f32[3,16,256]{2,1,0:T(8,128)S(1)}, f32[3,256,16,1024]{3,1,2,0:T(8,128)}) fusion(pred[256,1024]{1,0:T(8,128)(4,1)S(1)} %iota_compare_fusion.2, bf16[3,1024,1,64]{1,3,0,2:T(8,128)(2,1)S(1)} %get-tuple-element.149, bf16[3,1024,1,16,64]{1,4,3,0,2:T(8,128)(2,1)} %get-tuple-element.148, s32[]{:T(128)S(6)} %select_n.28), kind=kOutput, calls=%fused_computation.5.clone.1 | convolution fusion | flops 1648349184 | bytes 52609028 | tf_op jit(solution)/shard_map/while/body/eval_jaxpr/bqkgh,bskh->bkgqs/dot_general | solution.py:50
  582.6 21.8 %fusion.138 = f32[3,16,256]{2,1,0:T(8,128)S(1)} fusion(f32[3,256,16,1024]{3,1,2,0:T(8,128)} %get-tuple-element.123, f32[3,16,256]{2,1,0:T(8,128)S(1)} %get-tuple-element.124, pred[256,1024]{1,0:T(8,128)(4,1)S(1)} %iota_compare_fusion.2), kind=kLoop, calls=%fused_computation.4.clone.1 | loop fusion | flops 50319360 | bytes 50692096 | tf_op jit(solution)/shard_map/while/body/eval_jaxpr/reduce_sum | solution.py:55
  604.4 20.0 %fusion.139 = bf16[3,16,256,64]{2,3,1,0:T(8,128)(2,1)S(1)} fusion(f32[3,16,256]{2,1,0:T(8,128)S(1)} %fusion.138, f32[3,16,256]{2,1,0:T(8,128)S(1)} %get-tuple-element.124, f32[3,256,16,1024]{3,1,2,0:T(8,128)} %get-tuple-element.123, pred[256,1024]{1,0:T(8,128)(4,1)S(1)} %iota_compare_fusion.2, bf16[3,1024,1,64]{1,3,0,2:T(8,128)(2,1)S(1)} %copy-done.2), kind=kOutput, calls=%fused_computation.8.clone.1 | convolution fusion | flops 1674313728 | bytes 52658176 | tf_op jit(solution)/shard_map/while/body/eval_jaxpr/bkgqs,bskh->bqkgh/dot_general | solution.py:56
  624.4 1.2 constant_dynamic-update-slice_fusion.2
  625.6 62.1 %convolution_bitcast_fusion = f32[3,4,256,8192]{3,2,0,1:T(8,128)} fusion(bf16[4,3,256,1024]{2,3,1,0:T(8,128)(2,1)} %get-tuple-element.42, bf16[1024,8192]{1,0:T(8,128)(2,1)} %param.18), kind=kOutput, calls=%fused_computation.47 | convolution fusion | flops 51539607552 | bytes 123731968 | tf_op jit(solution)/shard_map/nbqc,cd->bnqd/dot_general | solution.py:60
  687.7 65.2 %copy.18 = f32[3,4,256,8192]{3,2,1,0:T(8,128)} copy(f32[3,4,256,8192]{3,2,0,1:T(8,128)} %convolution_bitcast_fusion) | data formatting | bytes 201326592 | tf_op jit(solution)/shard_map/nbqc,cd->bnqd/transpose | solution.py:60
  753.0 283.4 %fusion.80 = (u8[1024,4096]{1,0:T(8,128)(4,1)}, u8[1024,4096]{1,0:T(8,128)(4,1)}, f32[3,1024,4096]{2,1,0:T(8,128)}) fusion(bf16[3,1024,8192]{2,1,0:T(8,128)(2,1)} %all-gather.5.cloned.1.call-done, bf16[8192,4096]{1,0:T(8,128)(2,1)} %param.19), kind=kOutput, calls=%fused_computation.99 | convolution fusion | flops 206313619456 | bytes 176160768 | tf_op jit(solution)/shard_map/bsd,df->bsf/dot_general | solution.py:71
  1036.4 117.0 %fusion.128 = bf16[3,1024,4096]{2,1,0:T(8,128)(2,1)} fusion(f32[3,1024,4096]{2,1,0:T(8,128)} %get-tuple-element.83, u8[1024,4096]{1,0:T(8,128)(4,1)} %get-tuple-element.58, u8[1024,4096]{1,0:T(8,128)(4,1)} %get-tuple-element.57), kind=kLoop, calls=%fused_computation.28.clone.clone.1 | loop fusion | flops 880803840 | bytes 83886080 | tf_op jit(solution)/shard_map/bsf,fd->bsd/dot_general | solution.py:73
  1153.4 235.8 %bitcast_add_fusion = f32[3,1024,8192]{2,1,0:T(8,128)} fusion(f32[3,4,256,8192]{3,2,1,0:T(8,128)} %copy.18, bf16[4096,8192]{1,0:T(8,128)(2,1)} %param.20, bf16[3,1024,4096]{2,1,0:T(8,128)(2,1)} %fusion.128), kind=kOutput, calls=%fused_computation.20 | convolution fusion | flops 206183596032 | bytes 293601280 | tf_op jit(solution)/shard_map/bsf,fd->bsd/dot_general | solution.py:73
  1389.2 0.1 reduce-scatter.2.cloned.1.call-update
  1389.3 481.1 %reduce-scatter.2.cloned.1.call-done = f32[3,128,8192]{2,1,0:T(8,128)} async-done(((f32[3,1024,8192]{2,1,0:T(8,128)}), f32[3,128,8192]{2,1,0:T(8,128)}) %reduce-scatter.2.cloned.1.call-update) | async-done | bytes 12582928 | tf_op jit(solution)/shard_map/reduce_scatter | solution.py:74
  1870.3 11.1 fusion.76
  (11 shorter events, 0.0 us)
Async XLA Ops:
  6.5 244.5 %all-gather.3.cloned.1.call-start = ((), (), s32[]{:S(2)}) async-start(), calls=%async_computation.1 | async-start | bytes 56623104 | tf_op jit(solution)/shard_map/all_gather | solution.py:68
  24.1 728.9 %all-gather.5.cloned.1.call-start = ((), (), s32[]{:S(2)}) async-start(), calls=%async_computation.2 | async-start | bytes 56623104 | tf_op jit(solution)/shard_map/all_gather | solution.py:69
  24.9 1845.4 %reduce-scatter.2.cloned.1.call-start = ((), (), s32[]{:S(2)}) async-start(), calls=%async_computation.3 | async-start | bytes 113246208 | tf_op jit(solution)/shard_map/reduce_scatter | solution.py:74
  27.3 311.9 %copy-start = (f32[1024,64]{0,1:T(8,128)}, f32[1024,64]{0,1:T(8,128)S(1)}, u32[]{:S(2)}) copy-start(f32[1024,64]{0,1:T(8,128)S(1)} %get-tuple-element.81) | copy-start | bytes 786436
  27.3 311.9 %copy-start.1 = (f32[1024,64]{0,1:T(8,128)}, f32[1024,64]{0,1:T(8,128)S(1)}, u32[]{:S(2)}) copy-start(f32[1024,64]{0,1:T(8,128)S(1)} %get-tuple-element.82) | copy-start | bytes 786436
  369.4 41.7 %copy-start.2 = (bf16[3,1024,1,64]{1,3,0,2:T(8,128)(2,1)S(1)}, bf16[3,1024,1,64]{1,3,0,2:T(8,128)(2,1)}, u32[]{:S(2)}) copy-start(bf16[3,1024,1,64]{1,3,0,2:T(8,128)(2,1)} %get-tuple-element.150) | copy-start | bytes 1179652 | tf_op jit(solution)/shard_map/while
  433.8 41.7 %copy-start.2 = (bf16[3,1024,1,64]{1,3,0,2:T(8,128)(2,1)S(1)}, bf16[3,1024,1,64]{1,3,0,2:T(8,128)(2,1)}, u32[]{:S(2)}) copy-start(bf16[3,1024,1,64]{1,3,0,2:T(8,128)(2,1)} %get-tuple-element.150) | copy-start | bytes 1179652 | tf_op jit(solution)/shard_map/while
  498.2 41.7 %copy-start.2 = (bf16[3,1024,1,64]{1,3,0,2:T(8,128)(2,1)S(1)}, bf16[3,1024,1,64]{1,3,0,2:T(8,128)(2,1)}, u32[]{:S(2)}) copy-start(bf16[3,1024,1,64]{1,3,0,2:T(8,128)(2,1)} %get-tuple-element.150) | copy-start | bytes 1179652 | tf_op jit(solution)/shard_map/while
  562.7 41.7 %copy-start.2 = (bf16[3,1024,1,64]{1,3,0,2:T(8,128)(2,1)S(1)}, bf16[3,1024,1,64]{1,3,0,2:T(8,128)(2,1)}, u32[]{:S(2)}) copy-start(bf16[3,1024,1,64]{1,3,0,2:T(8,128)(2,1)} %get-tuple-element.150) | copy-start | bytes 1179652 | tf_op jit(solution)/shard_map/while
Sparse Core Ops, SparseCore 0:
  24.2 226.7 all-gather.2
  252.6 223.5 all-gather.4
  1389.4 480.9 reduce-scatter.1
where the time goes:
time: 1890 us
  matrix products  817 us (43%)
  waiting for transfers between devices  706 us (37%)
  other arithmetic  266 us (14%)
  local copies, waits for them, and re-layouts  83.1 us (4%)
    reduce_scatter x1, waiting for transfers between devices, local_layer(): lax.psum_scatter(attn_part + mlp_part, 'tp', scatter_dimension=1, tiled=T...  481 us
    dot_general x1, matrix products, local_layer(): jnp.einsum('bsd,df->bsf', mlp_in, w_up_part, preferred_element_type=jnp.f...  283 us
    dot_general x1, matrix products, local_layer(): jnp.einsum('bsf,fd->bsd', up_act, w_down_part, preferred_element_type=jnp...  236 us
    all_gather x1, waiting for transfers between devices, local_layer(): attn_in = lax.all_gather(normed_attn, 'tp', axis=1, tiled=True)  224 us
    dot_general x1, other arithmetic, local_layer(): jnp.einsum('bsf,fd->bsd', up_act, w_down_part, preferred_element_type=jnp...  117 us
    reduce_sum x4, other arithmetic, one_block(): jnp.sum(exp_scores, axis=-1, keepdims=True)  87 us
    dot_general x4, matrix products, one_block(): jnp.einsum('bkgqs,bskh->bqkgh', attn_probs, value_seq, preferred_element_...  79.9 us
    dot_general x4, matrix products, one_block(): jnp.einsum('bqkgh,bskh->bkgqs', query_blk, key_rot, preferred_element_typ...  79.8 us
  transfers between devices with their start and end apart: 3, of which 2 were waited for; matrix products, arithmetic and copies ran while one was open for 27% of the time, Pallas kernels for 0%

commit v1 on v0

v1 whole, which is shorter than its diff:
```python
import functools

import jax
import jax.numpy as jnp
from jax import lax
from jax.experimental import pallas as pl
from jax.experimental.pallas import tpu as pltpu
from jax.sharding import PartitionSpec as P

F32 = jnp.float32
BF16 = jnp.bfloat16
LANES = 128
ROWS = 64
NORM_GROUP = 16
VMEM_LIMIT = 67_000_000


def rotary_tables(positions, head_dim):
    inv_freq = 10000.0 ** (-2.0 * jnp.arange(head_dim // 2, dtype=F32) / head_dim)
    angles = positions.astype(F32)[:, None] * inv_freq[None, :]
    cos, sin = jnp.cos(angles), jnp.sin(angles)
    cos = jnp.concatenate([cos, cos], axis=-1)
    sin = jnp.concatenate([-sin, sin], axis=-1)
    q_tab = (jnp.concatenate([cos, cos], axis=-1), jnp.concatenate([sin, sin], axis=-1))
    kv_tab = (jnp.concatenate([cos, jnp.ones_like(cos)], axis=-1), jnp.concatenate([sin, jnp.zeros_like(sin)], axis=-1))
    return q_tab + kv_tab


def rotate(vals, cos, sin, first_half):
    half = LANES // 4
    vals = vals.astype(BF16).astype(F32)
    swapped = jnp.where(first_half, pltpu.roll(vals, LANES - half, 1), pltpu.roll(vals, half, 1))
    return (vals * cos + swapped * sin).astype(BF16)


def norm_rows(x_buf, a_buf, m_buf, gains, width, rows):
    group = NORM_GROUP
    chunks = width // LANES
    a_gain, a_bias, m_gain, m_bias = gains

    def one_group(g, carry):
        at = pl.ds(pl.multiple_of(g * group, group), group)
        parts = [jnp.zeros((group, LANES), F32) for _ in range(4)]
        for c in range(chunks):
            parts[c % 4] += x_buf[at, pl.ds(c * LANES, LANES)].astype(F32)
        mean = jnp.sum(parts[0] + parts[1] + (parts[2] + parts[3]), axis=-1, keepdims=True) * (1.0 / width)
        mean = jnp.broadcast_to(mean, (group, LANES))
        parts = [jnp.zeros((group, LANES), F32) for _ in range(4)]
        for c in range(chunks):
            d = x_buf[at, pl.ds(c * LANES, LANES)].astype(F32) - mean
            parts[c % 4] += d * d
        var = jnp.sum(parts[0] + parts[1] + (parts[2] + parts[3]), axis=-1, keepdims=True) * (1.0 / width)
        rstd = jnp.broadcast_to(lax.rsqrt(var + 1e-5), (group, LANES))
        for c in range(chunks):
            cols = pl.ds(c * LANES, LANES)
            n = (x_buf[at, cols].astype(F32) - mean) * rstd
            a_buf[at, cols] = (n * a_gain[:, cols] + a_bias[:, cols]).astype(BF16)
            m_buf[at, cols] = (n * m_gain[:, cols] + m_bias[:, cols]).astype(BF16)
        return carry

    lax.fori_loop(0, rows // group, one_group, 0)


def expand_kernel(devs, width, q_tiles, up_tiles, aliased, x_hbm, a_gain, a_bias, m_gain, m_bias, wq, wkv, wu, qc, qs, kc, ks, *refs):
    refs = refs[3:] if aliased else refs
    q_out, kv_out, act_out, x_buf, a_buf, m_buf, pend, sem = refs
    m, n = pl.program_id(0), pl.program_id(1)
    rows = devs * ROWS

    def fetch(tile, start):
        for d in range(devs):
            cp = pltpu.make_async_copy(
                x_hbm.at[d, pl.ds(tile * ROWS, ROWS)], x_buf.at[pl.ds(d * ROWS, ROWS)], sem)
            cp.start() if start else cp.wait()

    @pl.when((m == 0) & (n == 0))
    def _():
        fetch(0, True)

    @pl.when(n == 0)
    def _():
        fetch(m, False)
        norm_rows(x_buf, a_buf, m_buf, (a_gain, a_bias, m_gain, m_bias), width, rows)

    @pl.when((n == 1) & (m + 1 < pl.num_programs(0)))
    def _():
        fetch(m + 1, True)

    first_half = lax.rem(lax.broadcasted_iota(jnp.int32, (rows, LANES), 1), LANES // 2) < LANES // 4

    @pl.when(n < q_tiles)
    def _():
        acc = jnp.dot(a_buf[...], wq[...], preferred_element_type=F32)
        cos, sin = qc[...].reshape(rows, LANES), qs[...].reshape(rows, LANES)
        for c in range(acc.shape[1] // LANES):
            part = rotate(acc[:, c * LANES:(c + 1) * LANES], cos, sin, first_half)
            q_out[:, :, pl.ds(c * LANES, LANES)] = part.reshape(devs, ROWS, LANES)

    @pl.when(n == q_tiles)
    def _():
        acc = jnp.dot(a_buf[...], wkv[...], preferred_element_type=F32)
        cos, sin = kc[...].reshape(rows, LANES), ks[...].reshape(rows, LANES)
        kv_out[...] = rotate(acc, cos, sin, first_half).reshape(devs, ROWS, LANES)

    def gelu_out():
        u = pend[...]
        act = 0.5 * u * (1.0 + lax.erf(u * 0.7071067811865476))
        act_out[...] = act.astype(BF16).reshape(devs, ROWS, act.shape[1])

    def up_dot():
        pend[...] = jnp.dot(m_buf[...], wu[...], preferred_element_type=F32)

    @pl.when(n == q_tiles + 1)
    def _():
        up_dot()

    @pl.when((n > q_tiles + 1) & (n <= q_tiles + up_tiles))
    def _():
        gelu_out()
        up_dot()

    @pl.when(n == q_tiles + up_tiles + 1)
    def _():
        gelu_out()


def expand(xg, row0, seq_rows, norms, w_qkv, w_up, tabs, prev):
    devs, chunk, width = xg.shape
    q_cols = w_qkv.shape[1] - LANES
    up_cols = w_up.shape[1]
    tq, tu = min(256, q_cols), min(512, up_cols)
    q_tiles, up_tiles = q_cols // tq, up_cols // tu
    m_tiles = chunk // ROWS
    h0 = row0 // ROWS
    rows = devs * ROWS
    vec = pl.BlockSpec((1, width), lambda m, n: (0, 0))
    tab = pl.BlockSpec((devs, ROWS, LANES), lambda m, n: (0, h0 + m, 0))
    any_spec = pl.BlockSpec(memory_space=pl.ANY)
    in_specs = [
        any_spec, vec, vec, vec, vec,
        pl.BlockSpec((width, tq), lambda m, n: (0, jnp.minimum(n, q_tiles - 1))),
        pl.BlockSpec((width, LANES), lambda m, n: (0, q_cols // LANES)),
        pl.BlockSpec((width, tu), lambda m, n: (0, jnp.clip(n - q_tiles - 1, 0, up_tiles - 1))),
        tab, tab, tab, tab,
    ]
    args = [xg, *norms, w_qkv, w_qkv, w_up, *tabs]
    aliases = {}
    if prev is not None:
        aliases = {len(args) + k: k for k in range(3)}
        in_specs += [any_spec] * 3
        args += list(prev)
    out_shape = [jax.ShapeDtypeStruct((devs, seq_rows, c), BF16) for c in (q_cols, LANES, up_cols)]
    out_specs = [
        pl.BlockSpec((devs, ROWS, tq), lambda m, n: (0, h0 + m, jnp.minimum(n, q_tiles - 1))),
        pl.BlockSpec((devs, ROWS, LANES), lambda m, n: (0, h0 + m, 0)),
        pl.BlockSpec((devs, ROWS, tu), lambda m, n: (0, h0 + m, jnp.clip(n - q_tiles - 2, 0, up_tiles - 1))),
    ]
    flops = 2 * devs * chunk * width * (q_cols + LANES + up_cols)
    return pl.pallas_call(
        functools.partial(expand_kernel, devs, width, q_tiles, up_tiles, prev is not None),
        grid=(m_tiles, q_tiles + up_tiles + 2),
        in_specs=in_specs,
        out_specs=out_specs,
        out_shape=out_shape,
        scratch_shapes=[
            pltpu.VMEM((rows, width), BF16), pltpu.VMEM((rows, width), BF16), pltpu.VMEM((rows, width), BF16),
            pltpu.VMEM((rows, tu), F32), pltpu.SemaphoreType.DMA,
        ],
        input_output_aliases=aliases,
        compiler_params=pltpu.CompilerParams(vmem_limit_bytes=VMEM_LIMIT),
        cost_estimate=pl.CostEstimate(flops=flops, bytes_accessed=2 * width * (q_cols + up_cols), transcendentals=0),
        name="expand",
    )(*args)


def attend_kernel(seq, head_dim, q_ref, kv_ref, out_ref, k_lo, k_hi, v_lo, v_hi):
    scale = head_dim ** -0.5

    @pl.when(pl.program_id(0) == 0)
    def _():
        kv = kv_ref[...].astype(F32)
        low = lax.broadcasted_iota(jnp.int32, kv.shape, 1) < head_dim
        keys = jnp.where(low, kv, 0.0)
        vals = jnp.where(low, 0.0, kv)
        k_lo[...] = keys.astype(BF16)
        k_hi[...] = pltpu.roll(keys, head_dim, 1).astype(BF16)
        v_hi[...] = vals.astype(BF16)
        v_lo[...] = pltpu.roll(vals, head_dim, 1).astype(BF16)

    blk = min(256, seq)
    row = lax.broadcasted_iota(jnp.int32, (blk, blk), 0)
    col = lax.broadcasted_iota(jnp.int32, (blk, blk), 1)
    allowed = col <= row
    for b in range(seq // blk):
        q = q_ref[pl.ds(b * blk, blk), :]
        keys = (b + 1) * blk
        ctx = None
        for k_ref, v_ref in ((k_lo, v_lo), (k_hi, v_hi)):
            s = lax.dot_general(q, k_ref[pl.ds(0, keys), :], (((1,), (1,)), ((), ())), preferred_element_type=F32)
            diag = jnp.where(allowed, s[:, b * blk:], -1e30)
            s = diag if b == 0 else jnp.concatenate([s[:, :b * blk], diag], axis=1)
            e = jnp.exp((s - jnp.max(s, axis=-1, keepdims=True)) * scale)
            p = (e * (1.0 / jnp.sum(e, axis=-1, keepdims=True))).astype(BF16)
            part = jnp.dot(p, v_ref[pl.ds(0, keys), :], preferred_element_type=F32)
            ctx = part if ctx is None else ctx + part
        out_ref[pl.ds(b * blk, blk), :] = ctx.astype(BF16)


def attend(q, kv, head_dim):
    seq, q_cols = q.shape
    flops = 2 * seq * seq * q_cols * 4
    return pl.pallas_call(
        functools.partial(attend_kernel, seq, head_dim),
        grid=(q_cols // LANES,),
        in_specs=[pl.BlockSpec((seq, LANES), lambda h: (0, h)), pl.BlockSpec((seq, LANES), lambda h: (0, 0))],
        out_specs=pl.BlockSpec((seq, LANES), lambda h: (0, h)),
        out_shape=jax.ShapeDtypeStruct((seq, q_cols), BF16),
        scratch_shapes=[pltpu.VMEM((seq, LANES), BF16)] * 4,
        compiler_params=pltpu.CompilerParams(vmem_limit_bytes=VMEM_LIMIT),
        cost_estimate=pl.CostEstimate(flops=flops, bytes_accessed=4 * seq * q_cols, transcendentals=0),
        name="attend",
    )(q, kv)


def contract_kernel(num, final, steps, order, ctx_hbm, act_hbm, wo, wd, *refs):
    if final:
        add, far_lo, far_hi, up_lo, up_hi, down_lo, down_hi, own, ctx_buf, act_buf, sem = refs
    else:
        send_out, ctx_buf, act_buf, sem = refs
    blk = ctx_hbm.shape[1]
    j = pl.program_id(0)

    @pl.when(j == 0)
    def _():
        cps = []
        for k in range(num):
            rows = pl.ds(k * blk, blk)
            cps.append(pltpu.make_async_copy(ctx_hbm.at[order[k]], ctx_buf.at[rows], sem))
            cps.append(pltpu.make_async_copy(act_hbm.at[order[k]], act_buf.at[rows], sem))
        for cp in cps:
            cp.start()
        for cp in cps:
            cp.wait()

    acc = jnp.dot(act_buf[...], wd[...], preferred_element_type=F32)
    acc = acc + jnp.dot(ctx_buf[...], wo[...], preferred_element_type=F32)
    acc = acc.reshape(num, blk, acc.shape[1])
    if not final:
        send_out[...] = acc.astype(BF16)
        return
    acc = acc + add[...].astype(F32)
    own[...] = acc[3]

    @pl.when(j < steps // 2)
    def _():
        far_lo[...] = acc[0].astype(BF16)
        up_lo[...] = acc[1]
        down_lo[...] = acc[2].astype(BF16)

    @pl.when(j >= steps // 2)
    def _():
        far_hi[...] = acc[0].astype(BF16)
        up_hi[...] = acc[1].astype(BF16)
        down_hi[...] = acc[2]


def contract(order, ctx, act, w_out, w_down, col0, cols, add):
    num = order.shape[0]
    devs, blk, _ = ctx.shape
    tn = min(512, cols // 2)
    steps = cols // tn
    j0 = col0 // tn
    any_spec = pl.BlockSpec(memory_space=pl.ANY)
    in_specs = [
        any_spec, any_spec,
        pl.BlockSpec((w_out.shape[0], tn), lambda j, o: (0, j0 + j)),
        pl.BlockSpec((w_down.shape[0], tn), lambda j, o: (0, j0 + j)),
    ]
    args = [order, ctx, act, w_out, w_down]
    final = add is not None
    if final:
        in_specs.append(pl.BlockSpec((num, blk, tn), lambda j, o: (0, 0, j)))
        args.append(add)
        lo = pl.BlockSpec((blk, tn), lambda j, o: (0, jnp.minimum(j, steps // 2 - 1)))
        hi = pl.BlockSpec((blk, tn), lambda j, o: (0, jnp.maximum(j - steps // 2, 0)))
        half = lambda t: jax.ShapeDtypeStruct((blk, cols // 2), t)
        out_shape = [half(BF16), half(BF16), half(F32), half(BF16), half(BF16), half(F32), jax.ShapeDtypeStruct((blk, cols), F32)]
        out_specs = [lo, hi, lo, hi, lo, hi, pl.BlockSpec((blk, tn), lambda j, o: (0, j))]
    else:
        out_shape = jax.ShapeDtypeStruct((num, blk, cols), BF16)
        out_specs = pl.BlockSpec((num, blk, tn), lambda j, o: (0, 0, j))
    depth = w_out.shape[0] + w_down.shape[0]
    return pl.pallas_call(
        functools.partial(contract_kernel, num, final, steps),
        grid_spec=pltpu.PrefetchScalarGridSpec(
            num_scalar_prefetch=1,
            grid=(steps,),
            in_specs=in_specs,
            out_specs=out_specs,
            scratch_shapes=[
                pltpu.VMEM((num * blk, w_out.shape[0]), BF16), pltpu.VMEM((num * blk, w_down.shape[0]), BF16),
                pltpu.SemaphoreType.DMA,
            ],
        ),
        out_shape=out_shape,
        compiler_params=pltpu.CompilerParams(vmem_limit_bytes=VMEM_LIMIT),
        cost_estimate=pl.CostEstimate(flops=2 * num * blk * cols * depth, bytes_accessed=2 * depth * cols, transcendentals=0),
        name="contract_own" if final else "contract_pair",
    )(*args)


def schedule(batch, spans):
    steps = []
    steps.append(("attend", 0))
    for i in range(batch - 1):
        steps += [("pair", i), ("attend", i + 1)]
        if i:
            steps.append(("merge", i - 1))
        steps.append(("own", i))
    first = batch - 1
    steps += [("pair", first)]
    for i in range(first, spans):
        if i + 1 < spans:
            steps.append(("pair", i + 1))
        steps.append(("merge", i - 1))
        steps.append(("own", i))
        if i >= 2:
            steps.append(("finish", i - 2))
    return steps + [("finish", spans - 2), ("merge", spans - 1), ("finish", spans - 1)]


def solution(mesh):
    tp = mesh.shape["tp"]
    chips = tp // 2
    assert tp == 2 * chips and chips == 4
    pair = [(i, i ^ 1) for i in range(tp)]
    up_ring = [(i, (i + 2) % tp) for i in range(tp)]
    down_ring = [(i, (i - 2) % tp) for i in range(tp)]

    def local_layer(hidden_blk, attn_gain, attn_bias, mlp_gain, mlp_bias, w_qkv_part, w_out_part, w_up_part, w_down_part, positions):
        batch, seq_rows, width = hidden_blk.shape
        seq = seq_rows * tp
        w_qkv = w_qkv_part.reshape(width, w_qkv_part.shape[2])
        q_cols = w_out_part.shape[0]
        head_dim = (w_qkv.shape[1] - q_cols) // 2
        norms = [v.reshape(1, width) for v in (attn_gain, attn_bias, mlp_gain, mlp_bias)]
        tabs = [t.reshape(tp, seq_rows, LANES) for t in rotary_tables(positions, head_dim)]

        parts = []
        for b in range(batch):
            cut = [(0, seq_rows // 2), (seq_rows // 2, seq_rows)] if b == 0 else [(0, seq_rows)]
            parts += [(b, lo, hi) for lo, hi in cut]
        gathered = [lax.all_gather(hidden_blk[b, lo:hi], "tp", axis=0, tiled=False) for b, lo, hi in parts]

        last_done = [positions]

        def in_turn(first, *rest):
            out = lax.optimization_barrier((first, *rest, last_done[0]))
            return out[:-1] if rest else out[0]

        expanded = [None] * batch
        for (b, lo, hi), xg in zip(parts, gathered):
            expanded[b] = expand(in_turn(xg), lo, seq_rows, norms, w_qkv, w_up_part, tabs, expanded[b])
            last_done[0] = expanded[b][1]

        me = lax.axis_index("tp")
        chip, core = me // 2, me % 2
        targets = jnp.stack([(chip + 2) % chips, (chip + 1) % chips, (chip + chips - 1) % chips, chip]).astype(jnp.int32)
        own_order = targets * 2 + core
        pair_order = targets * 2 + (1 - core)
        ring_up = lambda v: lax.ppermute(v, "tp", up_ring)
        ring_down = lambda v: lax.ppermute(v, "tp", down_ring)

        spans = []
        for b in range(batch):
            col0 = 0
            for w in [width // 2, width // 4, width // 4] if b == batch - 1 else [width]:
                spans.append((b, col0, w))
                col0 += w
        ctxs, arrived, started, merged = {}, {}, {}, {}
        result = [jnp.zeros(hidden_blk.shape, BF16)]

        def run_attend(b):
            q, kv, act = expanded[b]
            q = in_turn(q)
            ctx = attend(q.reshape(seq, q_cols), kv.reshape(seq, LANES), head_dim)
            last_done[0] = ctx
            ctxs[b] = ctx.reshape(tp, seq_rows, q_cols)

        def run_pair(i):
            b, c, w = spans[i]
            send = contract(in_turn(pair_order), ctxs[b], expanded[b][2], w_out_part, w_down_part, c, w, None)
            last_done[0] = send
            arrived[i] = lax.ppermute(send, "tp", pair)

        def run_own(i):
            b, c, w = spans[i]
            far_lo, far_hi, up_lo, up_hi, down_lo, down_hi, own = contract(
                in_turn(own_order), ctxs[b], expanded[b][2], w_out_part, w_down_part, c, w, arrived[i])
            last_done[0] = far_lo
            started[i] = (ring_up(far_lo), ring_down(far_hi), ring_up(up_hi), ring_down(down_lo), up_lo, down_hi, own)

        def run_merge(i):
            from_below, from_above, up_hi, down_lo, up_lo, down_hi, own = started[i]
            up_lo = in_turn(up_lo)
            up_lo = (up_lo + from_below.astype(F32)).astype(BF16)
            down_hi = (down_hi + from_above.astype(F32)).astype(BF16)
            last_done[0] = up_lo
            merged[i] = (ring_up(up_lo), up_hi, down_lo, ring_down(down_hi), own)

        def run_finish(i):
            b, c, w = spans[i]
            up_lo, up_hi, down_lo, down_hi, own = merged[i]
            own = in_turn(own)
            half = w // 2
            for k, (up, down) in enumerate(((up_lo, down_lo), (up_hi, down_hi))):
                lo = k * half
                total = own[:, lo:lo + half] + (up.astype(F32) + down.astype(F32))
                rows = (hidden_blk[b, :, c + lo:c + lo + half].astype(F32) + total).astype(BF16)
                result[0] = lax.dynamic_update_slice(result[0], rows[None], (b, 0, c + lo))

        for step, arg in schedule(batch, len(spans)):
            {"attend": run_attend, "pair": run_pair, "own": run_own, "merge": run_merge, "finish": run_finish}[step](arg)
        return result[0]

    return jax.shard_map(
        local_layer, mesh=mesh,
        in_specs=(P("dp", "tp", None), P(), P(), P(), P(), P(None, "tp", None), P("tp", None), P(None, "tp"), P("tp", None), P()),
        out_specs=P("dp", "tp", None), check_vma=False)
```

time: 1890 us -> 1100 us (0.58)
  Pallas kernels: 0 us -> 866 us
  matrix products: 817 us -> 0 us
  waiting for transfers between devices: 706 us -> 118 us
  other arithmetic: 266 us -> 48.6 us
  local copies, waits for them, and re-layouts: 83.1 us -> 11.5 us
  starting transfers between devices: 0.65 us -> 36.6 us
    pallas_call x0 -> x17, Pallas kernels: none -> 866 us  [the longest x4 426 us: expand(): pl.pallas_call(functools.partial(expand_kernel, devs, width, q_tiles, up_...]
    dot_general x12 -> x0, matrix products: 817 us -> none  [the longest x1 283 us: local_layer(): jnp.einsum('bsd,df->bsf', mlp_in, w_up_part, preferred_element_type=jnp.f...]
    reduce_scatter x1 -> x0, waiting for transfers between devices: 481 us -> none  [local_layer(): lax.psum_scatter(attn_part + mlp_part, 'tp', scatter_dimension=1, tiled=T...]
    all_gather x2 -> x4, waiting for transfers between devices: 224 us -> 37.2 us  [local_layer(): lax.all_gather(hidden_blk[b, lo:hi], 'tp', axis=0, tiled=False)]
    dot_general x1 -> x0, other arithmetic: 117 us -> none  [local_layer(): jnp.einsum('bsf,fd->bsd', up_act, w_down_part, preferred_element_type=jnp...]
    reduce_sum x6 -> x0, other arithmetic: 95.3 us -> none  [the longest x4 87 us: one_block(): jnp.sum(exp_scores, axis=-1, keepdims=True)]
    ppermute x0 -> x35, waiting for transfers between devices: none -> 79.2 us  [the longest x15 73.1 us: local_layer(): ring_up = lambda v: lax.ppermute(v, 'tp', up_ring)]
    transpose x1 -> x0, local copies, waits for them, and re-layouts: 65.2 us -> none  [attention_branch(): jnp.einsum('nbqc,cd->bnqd', ctx_blocks, w_out_part, preferred_element_typ...]
  transfers between devices with their start and end apart: 3 -> 39, of which waited for: 2 -> 9; matrix products, arithmetic and copies ran while one was open for 27% -> 5% of each run, Pallas kernels for 0% -> 49%
where the time goes in v1:
time: 1100 us; the launch traced here: 1090 us
  Pallas kernels  866 us (79%)
  waiting for transfers between devices  118 us (11%)
  other arithmetic  48.6 us (4%)
  starting transfers between devices  36.6 us (3%)
  between operations  14.1 us (1%)
  local copies, waits for them, and re-layouts  11.5 us (1%)
    pallas_call x4, Pallas kernels, expand(): pl.pallas_call(functools.partial(expand_kernel, devs, width, q_tiles, up_...  426 us
    pallas_call x10, Pallas kernels, contract(): pl.pallas_call(functools.partial(contract_kernel, num, final, steps), gri...  358 us
    pallas_call x3, Pallas kernels, attend(): pl.pallas_call(functools.partial(attend_kernel, seq, head_dim), grid=(q_c...  81.5 us
    ppermute x15, waiting for transfers between devices, local_layer(): ring_up = lambda v: lax.ppermute(v, 'tp', up_ring)  73.1 us
    all_gather x4, waiting for transfers between devices, local_layer(): lax.all_gather(hidden_blk[b, lo:hi], 'tp', axis=0, tiled=False)  37.2 us
    ppermute x15, starting transfers between devices, local_layer(): ring_down = lambda v: lax.ppermute(v, 'tp', down_ring)  26.8 us
    dynamic_update_slice x9, other arithmetic, run_finish(): result[0] = lax.dynamic_update_slice(result[0], rows[None], (b, 0, c + lo))  23.6 us
  transfers between devices with their start and end apart: 39, of which 9 were waited for; matrix products, arithmetic and copies ran while one was open for 5% of the time, Pallas kernels for 49%

profile of v1, /device:TPU:112, one launch (start us, length us, event | category | flops | bytes accessed | tf_op | source)
XLA Modules:
  0.0 1094.0 jit_solution(10306424200303469041)
XLA Ops:
  6.6 3.1 fusion.33
  10.6 4.7 fusion.32
  16.9 1.9 fusion.31
  18.8 2.2 fusion.17
  21.0 37.1 %all-gather.9.cloned.1.call-done.x_hbm = bf16[8,64,8192]{2,1,0:T(8,128)(2,1)} async-done(((bf16[1,64,8192]{2,1,0:T(8,128)(2,1)}), bf16[8,64,8192]{2,1,0:T(8,128)(2,1)}) %all-gather.9.cloned.1.call-update) | async-done | bytes 8388624 | tf_op jit(solution)/shard_map/all_gather | solution.py:353
  58.1 72.0 %expand.4 = (bf16[8,128,1024]{2,1,0:T(8,128)(2,1)}, bf16[8,128,128]{2,1,0:T(8,128)(2,1)}, bf16[8,128,4096]{2,1,0:T(8,128)(2,1)}) custom-call(bf16[8,64,8192]{2,1,0:T(8,128)(2,1)} %all-gather.9.cloned.1.call-done.x_hbm, f32[1,8192]{1,0:T(1,128)} %bitcast.102, f32[1,8192]{1,0:T(1,128)} %bitcast.106, f32[1,8192]{1,0:T(1,128)} %bitcast.110, ...), custom_call_target="tpu_custom_call" | custom-call | flops 44023414784 | bytes 83886080 | tf_op jit(solution)/shard_map/expand/pallas_call | solution.py:159
  130.2 72.2 %expand.5 = (bf16[8,128,1024]{2,1,0:T(8,128)(2,1)}, bf16[8,128,128]{2,1,0:T(8,128)(2,1)}, bf16[8,128,4096]{2,1,0:T(8,128)(2,1)}) custom-call(bf16[8,64,8192]{2,1,0:T(8,128)(2,1)} %all-gather.7.cloned.1.call-done.x_hbm, f32[1,8192]{1,0:T(1,128)} %bitcast.103, f32[1,8192]{1,0:T(1,128)} %bitcast.107, ...), custom_call_target="tpu_custom_call", output_to_operand_aliasing={{0}: (12, {}), {1}: (13, {}), {2}: (14, {})} | custom-call | flops 44023414784 | bytes 83886080 | tf_op jit(solution)/shard_map/expand/pallas_call | solution.py:159
  202.5 140.6 %expand.6 = (bf16[8,128,1024]{2,1,0:T(8,128)(2,1)}, bf16[8,128,128]{2,1,0:T(8,128)(2,1)}, bf16[8,128,4096]{2,1,0:T(8,128)(2,1)}) custom-call(bf16[8,128,8192]{2,1,0:T(8,128)(2,1)} %all-gather.5.cloned.1.call-done.x_hbm, f32[1,8192]{1,0:T(1,128)} %bitcast.104, f32[1,8192]{1,0:T(1,128)} %bitcast.108, f32[1,8192]{1,0:T(1,128)} %bitcast.112, ...), custom_call_target="tpu_custom_call" | custom-call | flops 88046829568 | bytes 83886080 | tf_op jit(solution)/shard_map/expand/pallas_call | solution.py:159
  343.1 140.8 %expand.7 = (bf16[8,128,1024]{2,1,0:T(8,128)(2,1)}, bf16[8,128,128]{2,1,0:T(8,128)(2,1)}, bf16[8,128,4096]{2,1,0:T(8,128)(2,1)}) custom-call(bf16[8,128,8192]{2,1,0:T(8,128)(2,1)} %all-gather.11.cloned.1.call-done.x_hbm, f32[1,8192]{1,0:T(1,128)} %bitcast.105, f32[1,8192]{1,0:T(1,128)} %bitcast.109, f32[1,8192]{1,0:T(1,128)} %bitcast.113, ...), custom_call_target="tpu_custom_call" | custom-call | flops 88046829568 | bytes 83886080 | tf_op jit(solution)/shard_map/expand/pallas_call | solution.py:159
  483.9 27.2 %attend.3 = bf16[1024,1024]{1,0:T(8,128)(2,1)} custom-call(bf16[1024,1024]{1,0:T(8,128)(2,1)} %bitcast.124, bf16[1024,128]{1,0:T(8,128)(2,1)} %bitcast.127), custom_call_target="tpu_custom_call" | custom-call | flops 8589934592 | bytes 4194304 | tf_op jit(solution)/shard_map/attend/pallas_call | solution.py:212
  511.1 53.8 %contract_pair.5 = bf16[4,128,8192]{2,1,0:T(8,128)(2,1)} custom-call(s32[4]{0:T(128)} %get-tuple-element.120.order, bf16[8,128,1024]{2,1,0:T(8,128)(2,1)} %bitcast.122, bf16[8,128,4096]{2,1,0:T(8,128)(2,1)} %get-tuple-element.93.act_hbm, bf16[1024,8192]{1,0:T(8,128)(2,1)} %wo.19, bf16[4096,8192]{1,0:T(8,128)(2,1)} %wd.19), custom_call_target="tpu_custom_call" | custom-call | flops 42949672960 | bytes 83886080 | tf_op jit(solution)/shard_map/contract_pair/pallas_call | solution.py:293
  565.9 27.1 %attend.4 = bf16[1024,1024]{1,0:T(8,128)(2,1)} custom-call(bf16[1024,1024]{1,0:T(8,128)(2,1)} %bitcast.121, bf16[1024,128]{1,0:T(8,128)(2,1)} %bitcast.126), custom_call_target="tpu_custom_call" | custom-call | flops 8589934592 | bytes 4194304 | tf_op jit(solution)/shard_map/attend/pallas_call | solution.py:212
  593.0 55.6 %contract_own.5 = (bf16[128,4096]{1,0:T(8,128)(2,1)}, bf16[128,4096]{1,0:T(8,128)(2,1)}, f32[128,4096]{1,0:T(8,128)}, bf16[128,4096]{1,0:T(8,128)(2,1)}, bf16[12...) custom-call(s32[4]{0:T(128)} %broadcast_add_fusion.1.order, bf16[8,128,1024]{2,1,0:T(8,128)(2,1)} %bitcast.123, ...), custom_call_target="tpu_custom_call" | custom-call | flops 42949672960 | bytes 83886080 | tf_op jit(solution)/shard_map/contract_own/pallas_call | solution.py:293
  648.6 53.6 %contract_pair.6 = bf16[4,128,8192]{2,1,0:T(8,128)(2,1)} custom-call(s32[4]{0:T(128)} %get-tuple-element.120.order, bf16[8,128,1024]{2,1,0:T(8,128)(2,1)} %bitcast.118, bf16[8,128,4096]{2,1,0:T(8,128)(2,1)} %get-tuple-element.101.act_hbm, bf16[1024,8192]{1,0:T(8,128)(2,1)} %wo.19, bf16[4096,8192]{1,0:T(8,128)(2,1)} %wd.19), custom_call_target="tpu_custom_call" | custom-call | flops 42949672960 | bytes 83886080 | tf_op jit(solution)/shard_map/contract_pair/pallas_call | solution.py:293
  702.5 0.8 collective-permute-start.1
  703.3 27.2 %attend.5 = bf16[1024,1024]{1,0:T(8,128)(2,1)} custom-call(bf16[1024,1024]{1,0:T(8,128)(2,1)} %bitcast.120, bf16[1024,128]{1,0:T(8,128)(2,1)} %bitcast.125), custom_call_target="tpu_custom_call" | custom-call | flops 8589934592 | bytes 4194304 | tf_op jit(solution)/shard_map/attend/pallas_call | solution.py:212
  730.5 2.5 collective-permute-start.8
  732.9 3.1 add_convert_fusion.3
  736.0 55.9 %contract_own.6 = (bf16[128,4096]{1,0:T(8,128)(2,1)}, bf16[128,4096]{1,0:T(8,128)(2,1)}, f32[128,4096]{1,0:T(8,128)}, bf16[128,4096]{1,0:T(8,128)(2,1)}, bf16[12...) custom-call(s32[4]{0:T(128)} %broadcast_add_fusion.1.order, bf16[8,128,1024]{2,1,0:T(8,128)(2,1)} %bitcast.119, ...), custom_call_target="tpu_custom_call" | custom-call | flops 42949672960 | bytes 83886080 | tf_op jit(solution)/shard_map/contract_own/pallas_call | solution.py:293
  791.9 30.4 %contract_pair.7 = bf16[4,128,4096]{2,1,0:T(8,128)(2,1)} custom-call(s32[4]{0:T(128)} %get-tuple-element.120.order, bf16[8,128,1024]{2,1,0:T(8,128)(2,1)} %bitcast.88, bf16[8,128,4096]{2,1,0:T(8,128)(2,1)} %get-tuple-element.108.act_hbm, bf16[1024,8192]{1,0:T(8,128)(2,1)} %wo.19, bf16[4096,8192]{1,0:T(8,128)(2,1)} %wd.19), custom_call_target="tpu_custom_call" | custom-call | flops 21474836480 | bytes 41943040 | tf_op jit(solution)/shard_map/contract_pair/pallas_call | solution.py:293
  822.5 2.0 collective-permute-start.7
  824.5 3.1 add_convert_fusion.1
  827.6 3.2 collective-permute-start.15
  830.8 18.8 %contract_pair.8 = bf16[4,128,2048]{2,1,0:T(8,128)(2,1)} custom-call(s32[4]{0:T(128)} %get-tuple-element.120.order, bf16[8,128,1024]{2,1,0:T(8,128)(2,1)} %bitcast.89, bf16[8,128,4096]{2,1,0:T(8,128)(2,1)} %get-tuple-element.108.act_hbm, bf16[1024,8192]{1,0:T(8,128)(2,1)} %wo.19, bf16[4096,8192]{1,0:T(8,128)(2,1)} %wd.19), custom_call_target="tpu_custom_call" | custom-call | flops 10737418240 | bytes 20971520 | tf_op jit(solution)/shard_map/contract_pair/pallas_call | solution.py:293
  849.6 22.0 %collective-permute-done.3 = bf16[128,4096]{1,0:T(8,128)(2,1)} collective-permute-done((bf16[128,4096]{1,0:T(8,128)(2,1)}, bf16[128,4096]{1,0:T(8,128)(2,1)}, u32[]{:S(2)}, u32[]{:S(2)}) %collective-permute-start.3) | collective-permute-done | bytes 1048608 | tf_op jit(solution)/shard_map/ppermute | solution.py:371
  872.1 3.0 add_convert_fusion.2
  875.2 2.7 collective-permute-start.9
  877.9 2.5 add_convert_fusion
  880.3 31.7 %contract_own.7 = (bf16[128,2048]{1,0:T(8,128)(2,1)}, bf16[128,2048]{1,0:T(8,128)(2,1)}, f32[128,2048]{1,0:T(8,128)}, bf16[128,2048]{1,0:T(8,128)(2,1)}, bf16[12...) custom-call(s32[4]{0:T(128)} %broadcast_add_fusion.1.order, bf16[8,128,1024]{2,1,0:T(8,128)(2,1)} %bitcast.90, ...), custom_call_target="tpu_custom_call" | custom-call | flops 21474836480 | bytes 41943040 | tf_op jit(solution)/shard_map/contract_own/pallas_call | solution.py:293
  912.2 2.0 collective-permute-start.14
  914.2 3.0 fusion.4
  917.2 3.4 dynamic_update_slice.30
  920.8 3.4 fusion.6
  924.2 18.8 %contract_pair.9 = bf16[4,128,2048]{2,1,0:T(8,128)(2,1)} custom-call(s32[4]{0:T(128)} %get-tuple-element.120.order, bf16[8,128,1024]{2,1,0:T(8,128)(2,1)} %bitcast.91, bf16[8,128,4096]{2,1,0:T(8,128)(2,1)} %get-tuple-element.108.act_hbm, bf16[1024,8192]{1,0:T(8,128)(2,1)} %wo.19, bf16[4096,8192]{1,0:T(8,128)(2,1)} %wd.19), custom_call_target="tpu_custom_call" | custom-call | flops 10737418240 | bytes 20971520 | tf_op jit(solution)/shard_map/contract_pair/pallas_call | solution.py:293
  943.0 29.7 %collective-permute-done.10 = bf16[128,2048]{1,0:T(8,128)(2,1)} collective-permute-done((bf16[128,2048]{1,0:T(8,128)(2,1)}, bf16[128,2048]{1,0:T(8,128)(2,1)}, u32[]{:S(2)}, u32[]{:S(2)}) %collective-permute-start.10) | collective-permute-done | bytes 524320 | tf_op jit(solution)/shard_map/ppermute | solution.py:371
  972.7 2.3 add_convert_fusion.5
  975.1 20.0 %contract_own.8 = (bf16[128,1024]{1,0:T(8,128)(2,1)}, bf16[128,1024]{1,0:T(8,128)(2,1)}, f32[128,1024]{1,0:T(8,128)}, bf16[128,1024]{1,0:T(8,128)(2,1)}, bf16[12...) custom-call(s32[4]{0:T(128)} %broadcast_add_fusion.1.order, bf16[8,128,1024]{2,1,0:T(8,128)(2,1)} %bitcast.92, ...), custom_call_target="tpu_custom_call" | custom-call | flops 10737418240 | bytes 20971520 | tf_op jit(solution)/shard_map/contract_own/pallas_call | solution.py:293
  995.1 1.4 collective-permute-start.22
  996.5 1.7 collective-permute-start.20
  998.3 4.0 fusion.8
  1002.7 0.8 collective-permute-start.17
  1003.5 3.4 fusion.10
  1006.9 3.1 collective-permute-done.22
  1010.0 2.5 collective-permute-start.27
  1012.5 0.9 add_convert_fusion.4
  1013.4 9.5 collective-permute-done.17
  1023.0 0.8 add_convert_fusion.9
  1023.7 2.9 collective-permute-done.27
  1026.7 2.2 collective-permute-start.23
  1028.9 0.8 add_convert_fusion.8
  1030.2 19.8 %contract_own.9 = (bf16[128,1024]{1,0:T(8,128)(2,1)}, bf16[128,1024]{1,0:T(8,128)(2,1)}, f32[128,1024]{1,0:T(8,128)}, bf16[128,1024]{1,0:T(8,128)(2,1)}, bf16[12...) custom-call(s32[4]{0:T(128)} %broadcast_add_fusion.1.order, bf16[8,128,1024]{2,1,0:T(8,128)(2,1)} %bitcast.93, ...), custom_call_target="tpu_custom_call" | custom-call | flops 10737418240 | bytes 20971520 | tf_op jit(solution)/shard_map/contract_own/pallas_call | solution.py:293
  1050.1 1.6 collective-permute-start.26
  1051.8 2.7 fusion.14
  1054.5 3.2 collective-permute-start.28
  1057.8 2.7 fusion.16
  1060.5 3.2 collective-permute-start.33
  1063.7 2.5 collective-permute-done.24
  1066.6 1.9 fusion.24
  1068.5 1.6 collective-permute-done.29
  1070.7 1.8 fusion.26
  1072.6 3.0 collective-permute-start.34
  1075.6 7.8 collective-permute-done.30
  1083.4 1.8 fusion.28
  1085.2 1.8 fusion.30
  (102 shorter events, 6.9 us)
Async XLA Ops:
  6.5 51.6 %all-gather.9.cloned.1.call-start = ((), (), s32[]{:S(2)}) async-start(), calls=%async_computation.2 | async-start | bytes 9437184 | tf_op jit(solution)/shard_map/all_gather | solution.py:353
  9.7 120.5 %all-gather.7.cloned.1.call-start = ((), (), s32[]{:S(2)}) async-start(), calls=%async_computation.1 | async-start | bytes 9437184 | tf_op jit(solution)/shard_map/all_gather | solution.py:353
  10.5 191.9 %all-gather.5.cloned.1.call-start = ((), (), s32[]{:S(2)}) async-start(), calls=%async_computation | async-start | bytes 18874368 | tf_op jit(solution)/shard_map/all_gather | solution.py:353
  15.3 1.6 copy-start.10
  15.4 327.7 %all-gather.11.cloned.1.call-start = ((), (), s32[]{:S(2)}) async-start(), calls=%async_computation.3 | async-start | bytes 18874368 | tf_op jit(solution)/shard_map/all_gather | solution.py:353
  511.1 54.2 %copy-start.11 = (s32[4]{0:T(128)S(1)}, s32[4]{0:T(128)}, u32[]{:S(2)}) copy-start(s32[4]{0:T(128)} %get-tuple-element.154) | copy-start | bytes 52
  565.0 28.0 %collective-permute-start = (bf16[4,128,8192]{2,1,0:T(8,128)(2,1)}, bf16[4,128,8192]{2,1,0:T(8,128)(2,1)}, u32[]{:S(2)}, u32[]{:S(2)}) collective-permute-start(bf16[4,128,8192]{2,1,0:T(8,128)(2,1)} %contract_pair.5), channel_id=1, source_target_pairs={{0,1},{1,0},{2,3},{3,2},{4,5},{5,4},{6,7},{7,6},{8,9},{9,8},{10,11... | collective-permute-start | bytes 25165832 | tf_op jit(solution)/shard_map/ppermute | solution.py:394
  702.2 33.8 %collective-permute-start.2 = (bf16[4,128,8192]{2,1,0:T(8,128)(2,1)}, bf16[4,128,8192]{2,1,0:T(8,128)(2,1)}, u32[]{:S(2)}, u32[]{:S(2)}) collective-permute-start(bf16[4,128,8192]{2,1,0:T(8,128)(2,1)} %contract_pair.6), channel_id=1, source_target_pairs={{0,1},{1,0},{2,3},{3,2},{4,5},{5,4},{6,7},{7,6},{8,9},{9,8},{10,11... | collective-permute-start | bytes 25165832 | tf_op jit(solution)/shard_map/ppermute | solution.py:394
  702.5 30.4 %collective-permute-start.1 = (bf16[128,4096]{1,0:T(8,128)(2,1)}, bf16[128,4096]{1,0:T(8,128)(2,1)}, u32[]{:S(2)}, u32[]{:S(2)}) collective-permute-start(bf16[128,4096]{1,0:T(8,128)(2,1)} %get-tuple-element.99), channel_id=1, source_target_pairs={{0,2},{1,3},{2,4},{3,5},{4,6},{5,7},{6,0},{7,1},{8,10},{9,11},{10,... | collective-permute-start | bytes 3145736 | tf_op jit(solution)/shard_map/ppermute | solution.py:371
  730.5 94.0 %collective-permute-start.8 = (bf16[128,4096]{1,0:T(8,128)(2,1)}, bf16[128,4096]{1,0:T(8,128)(2,1)}, u32[]{:S(2)}, u32[]{:S(2)}) collective-permute-start(bf16[128,4096]{1,0:T(8,128)(2,1)} %get-tuple-element.117), channel_id=1, source_target_pairs={{0,6},{1,7},{2,0},{3,1},{4,2},{5,3},{6,4},{7,5},{8,14},{9,15},{10,... | collective-permute-start | bytes 3145736 | tf_op jit(solution)/shard_map/ppermute | solution.py:372
  822.3 58.1 %collective-permute-start.4 = (bf16[4,128,4096]{2,1,0:T(8,128)(2,1)}, bf16[4,128,4096]{2,1,0:T(8,128)(2,1)}, u32[]{:S(2)}, u32[]{:S(2)}) collective-permute-start(bf16[4,128,4096]{2,1,0:T(8,128)(2,1)} %contract_pair.7), channel_id=1, source_target_pairs={{0,1},{1,0},{2,3},{3,2},{4,5},{5,4},{6,7},{7,6},{8,9},{9,8},{10,11... | collective-permute-start | bytes 12582920 | tf_op jit(solution)/shard_map/ppermute | solution.py:394
  822.4 89.7 %collective-permute-start.6 = (bf16[128,4096]{1,0:T(8,128)(2,1)}, bf16[128,4096]{1,0:T(8,128)(2,1)}, u32[]{:S(2)}, u32[]{:S(2)}) collective-permute-start(bf16[128,4096]{1,0:T(8,128)(2,1)} %get-tuple-element.114), channel_id=1, source_target_pairs={{0,6},{1,7},{2,0},{3,1},{4,2},{5,3},{6,4},{7,5},{8,14},{9,15},{10,... | collective-permute-start | bytes 3145736 | tf_op jit(solution)/shard_map/ppermute | solution.py:372
  822.5 98.2 %collective-permute-start.7 = (bf16[128,4096]{1,0:T(8,128)(2,1)}, bf16[128,4096]{1,0:T(8,128)(2,1)}, u32[]{:S(2)}, u32[]{:S(2)}) collective-permute-start(bf16[128,4096]{1,0:T(8,128)(2,1)} %get-tuple-element.115), channel_id=1, source_target_pairs={{0,2},{1,3},{2,4},{3,5},{4,6},{5,7},{6,0},{7,1},{8,10},{9,11},{10,... | collective-permute-start | bytes 3145736 | tf_op jit(solution)/shard_map/ppermute | solution.py:371
  824.5 47.1 %collective-permute-start.3 = (bf16[128,4096]{1,0:T(8,128)(2,1)}, bf16[128,4096]{1,0:T(8,128)(2,1)}, u32[]{:S(2)}, u32[]{:S(2)}) collective-permute-start(bf16[128,4096]{1,0:T(8,128)(2,1)} %get-tuple-element.106), channel_id=1, source_target_pairs={{0,2},{1,3},{2,4},{3,5},{4,6},{5,7},{6,0},{7,1},{8,10},{9,11},{10,... | collective-permute-start | bytes 3145736 | tf_op jit(solution)/shard_map/ppermute | solution.py:371
  827.6 47.6 %collective-permute-start.15 = (bf16[128,4096]{1,0:T(8,128)(2,1)}, bf16[128,4096]{1,0:T(8,128)(2,1)}, u32[]{:S(2)}, u32[]{:S(2)}) collective-permute-start(bf16[128,4096]{1,0:T(8,128)(2,1)} %get-tuple-element.128), channel_id=1, source_target_pairs={{0,6},{1,7},{2,0},{3,1},{4,2},{5,3},{6,4},{7,5},{8,14},{9,15},{10,... | collective-permute-start | bytes 3145736 | tf_op jit(solution)/shard_map/ppermute | solution.py:372
  849.6 28.3 %copy-start.2 = (f32[128,4096]{1,0:T(8,128)S(1)}, f32[128,4096]{1,0:T(8,128)}, u32[]{:S(2)}) copy-start(f32[128,4096]{1,0:T(8,128)} %get-tuple-element.127) | copy-start | bytes 6291460
  871.6 40.6 %collective-permute-start.5 = (bf16[128,4096]{1,0:T(8,128)(2,1)}, bf16[128,4096]{1,0:T(8,128)(2,1)}, u32[]{:S(2)}, u32[]{:S(2)}) collective-permute-start(bf16[128,4096]{1,0:T(8,128)(2,1)} %add_convert_fusion.3), channel_id=1, source_target_pairs={{0,2},{1,3},{2,4},{3,5},{4,6},{5,7},{6,0},{7,1},{8,10},{9,11},{10,... | collective-permute-start | bytes 3145736 | tf_op jit(solution)/shard_map/ppermute | solution.py:371
  875.2 45.5 %collective-permute-start.9 = (bf16[128,4096]{1,0:T(8,128)(2,1)}, bf16[128,4096]{1,0:T(8,128)(2,1)}, u32[]{:S(2)}, u32[]{:S(2)}) collective-permute-start(bf16[128,4096]{1,0:T(8,128)(2,1)} %add_convert_fusion.1), channel_id=1, source_target_pairs={{0,6},{1,7},{2,0},{3,1},{4,2},{5,3},{6,4},{7,5},{8,14},{9,15},{10,... | collective-permute-start | bytes 3145736 | tf_op jit(solution)/shard_map/ppermute | solution.py:372
  880.3 94.7 %collective-permute-start.11 = (bf16[4,128,2048]{2,1,0:T(8,128)(2,1)}, bf16[4,128,2048]{2,1,0:T(8,128)(2,1)}, u32[]{:S(2)}, u32[]{:S(2)}) collective-permute-start(bf16[4,128,2048]{2,1,0:T(8,128)(2,1)} %contract_pair.8), channel_id=1, source_target_pairs={{0,1},{1,0},{2,3},{3,2},{4,5},{5,4},{6,7},{7,6},{8,9},{9,8},{10,11... | collective-permute-start | bytes 6291464 | tf_op jit(solution)/shard_map/ppermute | solution.py:394
  912.1 83.1 %collective-permute-start.13 = (bf16[128,4096]{1,0:T(8,128)(2,1)}, bf16[128,4096]{1,0:T(8,128)(2,1)}, u32[]{:S(2)}, u32[]{:S(2)}) collective-permute-start(bf16[128,4096]{1,0:T(8,128)(2,1)} %get-tuple-element.125), channel_id=1, source_target_pairs={{0,6},{1,7},{2,0},{3,1},{4,2},{5,3},{6,4},{7,5},{8,14},{9,15},{10,... | collective-permute-start | bytes 3145736 | tf_op jit(solution)/shard_map/ppermute | solution.py:372
  912.2 90.1 %collective-permute-start.14 = (bf16[128,4096]{1,0:T(8,128)(2,1)}, bf16[128,4096]{1,0:T(8,128)(2,1)}, u32[]{:S(2)}, u32[]{:S(2)}) collective-permute-start(bf16[128,4096]{1,0:T(8,128)(2,1)} %get-tuple-element.126), channel_id=1, source_target_pairs={{0,2},{1,3},{2,4},{3,5},{4,6},{5,7},{6,0},{7,1},{8,10},{9,11},{10,... | collective-permute-start | bytes 3145736 | tf_op jit(solution)/shard_map/ppermute | solution.py:371
  917.2 3.6 copy-start.1
  920.7 75.9 %collective-permute-start.12 = (bf16[128,4096]{1,0:T(8,128)(2,1)}, bf16[128,4096]{1,0:T(8,128)(2,1)}, u32[]{:S(2)}, u32[]{:S(2)}) collective-permute-start(bf16[128,4096]{1,0:T(8,128)(2,1)} %add_convert_fusion.2), channel_id=1, source_target_pairs={{0,2},{1,3},{2,4},{3,5},{4,6},{5,7},{6,0},{7,1},{8,10},{9,11},{10,... | collective-permute-start | bytes 3145736 | tf_op jit(solution)/shard_map/ppermute | solution.py:371
  920.7 52.1 %collective-permute-start.10 = (bf16[128,2048]{1,0:T(8,128)(2,1)}, bf16[128,2048]{1,0:T(8,128)(2,1)}, u32[]{:S(2)}, u32[]{:S(2)}) collective-permute-start(bf16[128,2048]{1,0:T(8,128)(2,1)} %get-tuple-element.112), channel_id=1, source_target_pairs={{0,2},{1,3},{2,4},{3,5},{4,6},{5,7},{6,0},{7,1},{8,10},{9,11},{10,... | collective-permute-start | bytes 1572872 | tf_op jit(solution)/shard_map/ppermute | solution.py:371
  972.7 29.9 %collective-permute-start.16 = (bf16[128,4096]{1,0:T(8,128)(2,1)}, bf16[128,4096]{1,0:T(8,128)(2,1)}, u32[]{:S(2)}, u32[]{:S(2)}) collective-permute-start(bf16[128,4096]{1,0:T(8,128)(2,1)} %add_convert_fusion), channel_id=1, source_target_pairs={{0,6},{1,7},{2,0},{3,1},{4,2},{5,3},{6,4},{7,5},{8,14},{9,15},{10,... | collective-permute-start | bytes 3145736 | tf_op jit(solution)/shard_map/ppermute | solution.py:372
  975.1 54.6 %collective-permute-start.18 = (bf16[4,128,2048]{2,1,0:T(8,128)(2,1)}, bf16[4,128,2048]{2,1,0:T(8,128)(2,1)}, u32[]{:S(2)}, u32[]{:S(2)}) collective-permute-start(bf16[4,128,2048]{2,1,0:T(8,128)(2,1)} %contract_pair.9), channel_id=1, source_target_pairs={{0,1},{1,0},{2,3},{3,2},{4,5},{5,4},{6,7},{7,6},{8,9},{9,8},{10,11... | collective-permute-start | bytes 6291464 | tf_op jit(solution)/shard_map/ppermute | solution.py:394
  995.1 7.6 copy-start.16
  995.1 8.4 copy-start
  995.1 14.9 %collective-permute-start.22 = (bf16[128,2048]{1,0:T(8,128)(2,1)}, bf16[128,2048]{1,0:T(8,128)(2,1)S(1)}, u32[]{:S(2)}, u32[]{:S(2)}) collective-permute-start(bf16[128,2048]{1,0:T(8,128)(2,1)} %get-tuple-element.138), channel_id=1, source_target_pairs={{0,6},{1,7},{2,0},{3,1},{4,2},{5,3},{6,4},{7,5},{8,14},{9,15},{10,... | collective-permute-start | bytes 1572872 | tf_op jit(solution)/shard_map/ppermute | solution.py:372
  996.5 53.6 %collective-permute-start.20 = (bf16[128,2048]{1,0:T(8,128)(2,1)}, bf16[128,2048]{1,0:T(8,128)(2,1)}, u32[]{:S(2)}, u32[]{:S(2)}) collective-permute-start(bf16[128,2048]{1,0:T(8,128)(2,1)} %get-tuple-element.135), channel_id=1, source_target_pairs={{0,6},{1,7},{2,0},{3,1},{4,2},{5,3},{6,4},{7,5},{8,14},{9,15},{10,... | collective-permute-start | bytes 1572872 | tf_op jit(solution)/shard_map/ppermute | solution.py:372
  1002.3 7.8 copy-start.15
  1002.3 10.3 copy-start.5
  1002.3 20.7 %copy-start.9 = (f32[128,1024]{1,0:T(8,128)S(1)}, f32[128,1024]{1,0:T(8,128)}, u32[]{:S(2)}) copy-start(f32[128,1024]{1,0:T(8,128)} %get-tuple-element.131) | copy-start | bytes 1572868
  1002.3 26.6 %copy-start.8 = (f32[128,1024]{1,0:T(8,128)S(1)}, f32[128,1024]{1,0:T(8,128)}, u32[]{:S(2)}) copy-start(f32[128,1024]{1,0:T(8,128)} %get-tuple-element.143) | copy-start | bytes 1572868
  1002.3 52.2 %collective-permute-start.21 = (bf16[128,2048]{1,0:T(8,128)(2,1)}, bf16[128,2048]{1,0:T(8,128)(2,1)}, u32[]{:S(2)}, u32[]{:S(2)}) collective-permute-start(bf16[128,2048]{1,0:T(8,128)(2,1)} %get-tuple-element.136), channel_id=1, source_target_pairs={{0,2},{1,3},{2,4},{3,5},{4,6},{5,7},{6,0},{7,1},{8,10},{9,11},{10,... | collective-permute-start | bytes 1572872 | tf_op jit(solution)/shard_map/ppermute | solution.py:371
  1002.7 20.3 %collective-permute-start.17 = (bf16[128,1024]{1,0:T(8,128)(2,1)S(1)}, bf16[128,1024]{1,0:T(8,128)(2,1)S(1)}, u32[]{:S(2)}, u32[]{:S(2)}) collective-permute-start(bf16[128,1024]{1,0:T(8,128)(2,1)S(1)} %copy-done.16), channel_id=1, source_target_pairs={{0,2},{1,3},{2,4},{3,5},{4,6},{5,7},{6,0},{7,1},{8,10},{9,11},{10,... | collective-permute-start | bytes 786440 | tf_op jit(solution)/shard_map/ppermute | solution.py:371
  1010.0 16.7 %collective-permute-start.27 = (bf16[128,1024]{1,0:T(8,128)(2,1)S(1)}, bf16[128,1024]{1,0:T(8,128)(2,1)S(1)}, u32[]{:S(2)}, u32[]{:S(2)}) collective-permute-start(bf16[128,1024]{1,0:T(8,128)(2,1)S(1)} %copy-done.15), channel_id=1, source_target_pairs={{0,6},{1,7},{2,0},{3,1},{4,2},{5,3},{6,4},{7,5},{8,14},{9,15},{10,... | collective-permute-start | bytes 786440 | tf_op jit(solution)/shard_map/ppermute | solution.py:372
  1023.0 28.7 %collective-permute-start.19 = (bf16[128,2048]{1,0:T(8,128)(2,1)}, bf16[128,2048]{1,0:T(8,128)(2,1)}, u32[]{:S(2)}, u32[]{:S(2)}) collective-permute-start(bf16[128,2048]{1,0:T(8,128)(2,1)} %add_convert_fusion.5), channel_id=1, source_target_pairs={{0,2},{1,3},{2,4},{3,5},{4,6},{5,7},{6,0},{7,1},{8,10},{9,11},{10,... | collective-permute-start | bytes 1572872 | tf_op jit(solution)/shard_map/ppermute | solution.py:371
  1026.7 31.1 %collective-permute-start.23 = (bf16[128,2048]{1,0:T(8,128)(2,1)}, bf16[128,2048]{1,0:T(8,128)(2,1)}, u32[]{:S(2)}, u32[]{:S(2)}) collective-permute-start(bf16[128,2048]{1,0:T(8,128)(2,1)} %add_convert_fusion.4), channel_id=1, source_target_pairs={{0,6},{1,7},{2,0},{3,1},{4,2},{5,3},{6,4},{7,5},{8,14},{9,15},{10,... | collective-permute-start | bytes 1572872 | tf_op jit(solution)/shard_map/ppermute | solution.py:372
  1029.7 30.8 %collective-permute-start.25 = (bf16[128,1024]{1,0:T(8,128)(2,1)}, bf16[128,1024]{1,0:T(8,128)(2,1)}, u32[]{:S(2)}, u32[]{:S(2)}) collective-permute-start(bf16[128,1024]{1,0:T(8,128)(2,1)} %get-tuple-element.141), channel_id=1, source_target_pairs={{0,6},{1,7},{2,0},{3,1},{4,2},{5,3},{6,4},{7,5},{8,14},{9,15},{10,... | collective-permute-start | bytes 786440 | tf_op jit(solution)/shard_map/ppermute | solution.py:372
  1050.0 10.5 copy-start.14
  1050.1 16.1 %copy-start.13 = (bf16[128,1024]{1,0:T(8,128)(2,1)S(1)}, bf16[128,1024]{1,0:T(8,128)(2,1)}, u32[]{:S(2)}) copy-start(bf16[128,1024]{1,0:T(8,128)(2,1)} %get-tuple-element.149) | copy-start | bytes 786436
  1050.1 16.5 %copy-start.3 = (f32[128,2048]{1,0:T(8,128)S(1)}, f32[128,2048]{1,0:T(8,128)}, u32[]{:S(2)}) copy-start(f32[128,2048]{1,0:T(8,128)} %get-tuple-element.140) | copy-start | bytes 3145732
  1050.1 20.0 %copy-start.12 = (bf16[128,1024]{1,0:T(8,128)(2,1)S(1)}, bf16[128,1024]{1,0:T(8,128)(2,1)}, u32[]{:S(2)}) copy-start(bf16[128,1024]{1,0:T(8,128)(2,1)} %get-tuple-element.150) | copy-start | bytes 786436
  1050.1 20.1 %copy-start.7 = (f32[128,1024]{1,0:T(8,128)S(1)}, f32[128,1024]{1,0:T(8,128)}, u32[]{:S(2)}) copy-start(f32[128,1024]{1,0:T(8,128)} %get-tuple-element.147) | copy-start | bytes 1572868
  1050.1 20.2 %collective-permute-start.26 = (bf16[128,1024]{1,0:T(8,128)(2,1)}, bf16[128,1024]{1,0:T(8,128)(2,1)S(1)}, u32[]{:S(2)}, u32[]{:S(2)}) collective-permute-start(bf16[128,1024]{1,0:T(8,128)(2,1)} %get-tuple-element.142), channel_id=1, source_target_pairs={{0,2},{1,3},{2,4},{3,5},{4,6},{5,7},{6,0},{7,1},{8,10},{9,11},{10,... | collective-permute-start | bytes 786440 | tf_op jit(solution)/shard_map/ppermute | solution.py:371
  1051.7 14.5 %collective-permute-start.24 = (bf16[128,1024]{1,0:T(8,128)(2,1)}, bf16[128,1024]{1,0:T(8,128)(2,1)S(1)}, u32[]{:S(2)}, u32[]{:S(2)}) collective-permute-start(bf16[128,1024]{1,0:T(8,128)(2,1)} %add_convert_fusion.9), channel_id=1, source_target_pairs={{0,2},{1,3},{2,4},{3,5},{4,6},{5,7},{6,0},{7,1},{8,10},{9,11},{10,... | collective-permute-start | bytes 786440 | tf_op jit(solution)/shard_map/ppermute | solution.py:371
  1054.5 17.9 %copy-start.6 = (f32[128,1024]{1,0:T(8,128)S(1)}, f32[128,1024]{1,0:T(8,128)}, u32[]{:S(2)}) copy-start(f32[128,1024]{1,0:T(8,128)} %get-tuple-element.151) | copy-start | bytes 1572868
  1054.5 28.9 %copy-start.4 = (f32[128,2048]{1,0:T(8,128)S(1)}, f32[128,2048]{1,0:T(8,128)}, u32[]{:S(2)}) copy-start(f32[128,2048]{1,0:T(8,128)} %get-tuple-element.148) | copy-start | bytes 3145732
  1054.5 16.1 %collective-permute-start.28 = (bf16[128,1024]{1,0:T(8,128)(2,1)}, bf16[128,1024]{1,0:T(8,128)(2,1)S(1)}, u32[]{:S(2)}, u32[]{:S(2)}) collective-permute-start(bf16[128,1024]{1,0:T(8,128)(2,1)} %add_convert_fusion.8), channel_id=1, source_target_pairs={{0,6},{1,7},{2,0},{3,1},{4,2},{5,3},{6,4},{7,5},{8,14},{9,15},{10,... | collective-permute-start | bytes 786440 | tf_op jit(solution)/shard_map/ppermute | solution.py:372
  1057.8 12.3 %collective-permute-start.29 = (bf16[128,1024]{1,0:T(8,128)(2,1)}, bf16[128,1024]{1,0:T(8,128)(2,1)S(1)}, u32[]{:S(2)}, u32[]{:S(2)}) collective-permute-start(bf16[128,1024]{1,0:T(8,128)(2,1)} %get-tuple-element.133), channel_id=1, source_target_pairs={{0,2},{1,3},{2,4},{3,5},{4,6},{5,7},{6,0},{7,1},{8,10},{9,11},{10,... | collective-permute-start | bytes 786440 | tf_op jit(solution)/shard_map/ppermute | solution.py:371
  1060.5 12.0 %collective-permute-start.33 = (bf16[128,1024]{1,0:T(8,128)(2,1)S(1)}, bf16[128,1024]{1,0:T(8,128)(2,1)S(1)}, u32[]{:S(2)}, u32[]{:S(2)}) collective-permute-start(bf16[128,1024]{1,0:T(8,128)(2,1)S(1)} %copy-done.14), channel_id=1, source_target_pairs={{0,6},{1,7},{2,0},{3,1},{4,2},{5,3},{6,4},{7,5},{8,14},{9,15},{10,... | collective-permute-start | bytes 786440 | tf_op jit(solution)/shard_map/ppermute | solution.py:372
  1066.2 9.4 collective-permute-start.31
  1070.0 15.2 %collective-permute-start.32 = (bf16[128,1024]{1,0:T(8,128)(2,1)S(1)}, bf16[128,1024]{1,0:T(8,128)(2,1)S(1)}, u32[]{:S(2)}, u32[]{:S(2)}) collective-permute-start(bf16[128,1024]{1,0:T(8,128)(2,1)S(1)} %copy-done.12), channel_id=1, source_target_pairs={{0,2},{1,3},{2,4},{3,5},{4,6},{5,7},{6,0},{7,1},{8,10},{9,11},{10,... | collective-permute-start | bytes 786440 | tf_op jit(solution)/shard_map/ppermute | solution.py:371
  1070.3 13.1 %collective-permute-start.30 = (bf16[128,1024]{1,0:T(8,128)(2,1)S(1)}, bf16[128,1024]{1,0:T(8,128)(2,1)S(1)}, u32[]{:S(2)}, u32[]{:S(2)}) collective-permute-start(bf16[128,1024]{1,0:T(8,128)(2,1)S(1)} %add_convert_fusion.7), channel_id=1, source_target_pairs={{0,2},{1,3},{2,4},{3,5},{4,6},{5,7},{6,0},{7,1},{8,10},{9,11},{10,... | collective-permute-start | bytes 786440 | tf_op jit(solution)/shard_map/ppermute | solution.py:371
  1072.6 12.7 %collective-permute-start.34 = (bf16[128,1024]{1,0:T(8,128)(2,1)S(1)}, bf16[128,1024]{1,0:T(8,128)(2,1)S(1)}, u32[]{:S(2)}, u32[]{:S(2)}) collective-permute-start(bf16[128,1024]{1,0:T(8,128)(2,1)S(1)} %add_convert_fusion.6), channel_id=1, source_target_pairs={{0,6},{1,7},{2,0},{3,1},{4,2},{5,3},{6,4},{7,5},{8,14},{9,15},{10,... | collective-permute-start | bytes 786440 | tf_op jit(solution)/shard_map/ppermute | solution.py:372
Sparse Core Ops, SparseCore 0:
  9.8 48.2 all-gather.8
  59.7 45.6 all-gather.6
  107.0 81.2 all-gather.4
  189.8 81.6 all-gather.10

commit v2 on v1

v2 whole, which is shorter than its diff:
```python
import functools

import jax
import jax.numpy as jnp
from jax import lax
from jax.experimental import pallas as pl
from jax.experimental.pallas import tpu as pltpu
from jax.sharding import PartitionSpec as P


F32 = jnp.float32
BF16 = jnp.bfloat16
LANES = 128
ROWS = 64
VMEM_LIMIT = 67_000_000


def rotary_tables(positions, head_dim):
    inv_freq = 10000.0 ** (-2.0 * jnp.arange(head_dim // 2, dtype=F32) / head_dim)
    angles = positions.astype(F32)[:, None] * inv_freq[None, :]
    cos, sin = jnp.cos(angles), jnp.sin(angles)
    cos = jnp.concatenate([cos, cos], axis=-1)
    sin = jnp.concatenate([-sin, sin], axis=-1)
    q_tab = (jnp.concatenate([cos, cos], axis=-1), jnp.concatenate([sin, sin], axis=-1))
    kv_tab = (jnp.concatenate([cos, jnp.ones_like(cos)], axis=-1), jnp.concatenate([sin, jnp.zeros_like(sin)], axis=-1))
    return q_tab + kv_tab


def rotate(vals, cos, sin, first_half):
    half = LANES // 4
    vals = vals.astype(BF16).astype(F32)
    swapped = jnp.where(first_half, pltpu.roll(vals, LANES - half, 1), pltpu.roll(vals, half, 1))
    return (vals * cos + swapped * sin).astype(BF16)


def norm_rows(x_buf, out_buf, mean, rstd, gain, bias, start, count, width):
    at = pl.ds(start, count)
    for c in range(width // LANES):
        cols = pl.ds(c * LANES, LANES)
        n = (x_buf[at, cols].astype(F32) - mean) * rstd
        out_buf[at, cols] = (n * gain[:, cols] + bias[:, cols]).astype(BF16)


def expand_kernel(devs, width, q_tiles, up_tiles, aliased, x_hbm, mean_ref, rstd_ref, a_gain, a_bias, m_gain, m_bias, wq, wkv, wu, qc, qs, kc, ks, *refs):
    refs = refs[3:] if aliased else refs
    q_out, kv_out, act_out, x_buf, a_buf, m_buf, pend, stat, sems = refs
    m, n = pl.program_id(0), pl.program_id(1)
    rows = devs * ROWS

    def fetch(tile, d):
        return pltpu.make_async_copy(
            x_hbm.at[d, pl.ds(tile * ROWS, ROWS)], x_buf.at[pl.ds(d * ROWS, ROWS)], sems.at[d])

    def row_stats(start, count):
        at = pl.ds(start, count)
        return stat[0, at, :], stat[1, at, :]

    @pl.when((m == 0) & (n == 0))
    def _():
        for d in range(devs):
            fetch(0, d).start()

    @pl.when((n == 0) | (n == q_tiles + 2))
    def _():
        stat[0] = mean_ref[...].reshape(rows, LANES)
        stat[1] = rstd_ref[...].reshape(rows, LANES)

    @pl.when((m == 0) & (n == 0))
    def _():
        def one(d, carry):
            fetch(0, d).wait()
            start = pl.multiple_of(d * ROWS, ROWS)
            mean, rstd = row_stats(start, ROWS)
            norm_rows(x_buf, a_buf, mean, rstd, a_gain, a_bias, start, ROWS, width)
            return carry

        lax.fori_loop(0, devs, one, 0)

    @pl.when((n == q_tiles) & (m + 1 < pl.num_programs(0)))
    def _():
        for d in range(devs):
            fetch(m + 1, d).start()

    @pl.when((n == q_tiles + 2) & (m + 1 < pl.num_programs(0)))
    def _():
        for d in range(devs):
            fetch(m + 1, d).wait()

    first_half = lax.rem(lax.broadcasted_iota(jnp.int32, (rows, LANES), 1), LANES // 2) < LANES // 4

    @pl.when(n < q_tiles)
    def _():
        count = rows // q_tiles
        start = pl.multiple_of(n * count, count)
        mean, rstd = row_stats(start, count)
        norm_rows(x_buf, m_buf, mean, rstd, m_gain, m_bias, start, count, width)
        acc = jnp.dot(a_buf[...], wq[...], preferred_element_type=F32)
        cos, sin = qc[...].reshape(rows, LANES), qs[...].reshape(rows, LANES)
        for c in range(acc.shape[1] // LANES):
            part = rotate(acc[:, c * LANES:(c + 1) * LANES], cos, sin, first_half)
            q_out[:, :, pl.ds(c * LANES, LANES)] = part.reshape(devs, ROWS, LANES)

    @pl.when(n == q_tiles)
    def _():
        acc = jnp.dot(a_buf[...], wkv[...], preferred_element_type=F32)
        cos, sin = kc[...].reshape(rows, LANES), ks[...].reshape(rows, LANES)
        kv_out[...] = rotate(acc, cos, sin, first_half).reshape(devs, ROWS, LANES)

    def gelu_out():
        u = pend[...]
        act = 0.5 * u * (1.0 + lax.erf(u * 0.7071067811865476))
        act_out[...] = act.astype(BF16).reshape(devs, ROWS, act.shape[1])

    def up_dot():
        pend[...] = jnp.dot(m_buf[...], wu[...], preferred_element_type=F32)

    @pl.when(n == q_tiles + 1)
    def _():
        up_dot()

    @pl.when((n > q_tiles + 1) & (n <= q_tiles + up_tiles))
    def _():
        count = pl.cdiv(pl.cdiv(rows, up_tiles - 1), 16) * 16
        start = pl.multiple_of(jnp.minimum((n - q_tiles - 2) * count, rows - count), 16)
        mean, rstd = row_stats(start, count)
        norm_rows(x_buf, a_buf, mean, rstd, a_gain, a_bias, start, count, width)
        gelu_out()
        up_dot()

    @pl.when(n == q_tiles + up_tiles + 1)
    def _():
        gelu_out()


def expand(xg, batch_id, row0, seq_rows, stats, norms, w_qkv, w_up, tabs, prev):
    devs, chunk, width = xg.shape
    q_cols = w_qkv.shape[1] - LANES
    up_cols = w_up.shape[1]
    tq, tu = min(256, q_cols), min(512, up_cols)
    q_tiles, up_tiles = q_cols // tq, up_cols // tu
    m_tiles = chunk // ROWS
    h0 = row0 // ROWS
    rows = devs * ROWS
    vec = pl.BlockSpec((1, width), lambda m, n: (0, 0))
    tab = pl.BlockSpec((devs, ROWS, LANES), lambda m, n: (0, h0 + m, 0))
    any_spec = pl.BlockSpec(memory_space=pl.ANY)
    stat_specs = [
        pl.BlockSpec((None, None, devs, ROWS, LANES), lambda m, n, k=k: (
            k, batch_id, 0, h0 + jnp.minimum(m + (n > q_tiles).astype(jnp.int32), m_tiles - 1), 0))
        for k in range(2)
    ]
    in_specs = [
        any_spec, *stat_specs, vec, vec, vec, vec,
        pl.BlockSpec((width, tq), lambda m, n: (0, jnp.minimum(n, q_tiles - 1))),
        pl.BlockSpec((width, LANES), lambda m, n: (0, q_cols // LANES)),
        pl.BlockSpec((width, tu), lambda m, n: (0, jnp.clip(n - q_tiles - 1, 0, up_tiles - 1))),
        tab, tab, tab, tab,
    ]
    args = [xg, stats, stats, *norms, w_qkv, w_qkv, w_up, *tabs]
    aliases = {}
    if prev is not None:
        aliases = {len(args) + k: k for k in range(3)}
        in_specs += [any_spec] * 3
        args += list(prev)
    out_shape = [jax.ShapeDtypeStruct((devs, seq_rows, c), BF16) for c in (q_cols, LANES, up_cols)]
    out_specs = [
        pl.BlockSpec((devs, ROWS, tq), lambda m, n: (0, h0 + m, jnp.minimum(n, q_tiles - 1))),
        pl.BlockSpec((devs, ROWS, LANES), lambda m, n: (0, h0 + m, 0)),
        pl.BlockSpec((devs, ROWS, tu), lambda m, n: (0, h0 + m, jnp.clip(n - q_tiles - 2, 0, up_tiles - 1))),
    ]
    flops = 2 * devs * chunk * width * (q_cols + LANES + up_cols)
    return pl.pallas_call(
        functools.partial(expand_kernel, devs, width, q_tiles, up_tiles, prev is not None),
        grid=(m_tiles, q_tiles + up_tiles + 2),
        in_specs=in_specs,
        out_specs=out_specs,
        out_shape=out_shape,
        scratch_shapes=[
            pltpu.VMEM((rows, width), BF16), pltpu.VMEM((rows, width), BF16), pltpu.VMEM((rows, width), BF16),
            pltpu.VMEM((rows, tu), F32), pltpu.VMEM((2, rows, LANES), F32), pltpu.SemaphoreType.DMA((devs,)),
        ],
        input_output_aliases=aliases,
        compiler_params=pltpu.CompilerParams(vmem_limit_bytes=VMEM_LIMIT),
        cost_estimate=pl.CostEstimate(flops=flops, bytes_accessed=2 * width * (q_cols + up_cols), transcendentals=0),
        name="expand",
    )(*args)


def attend_kernel(seq, head_dim, q_ref, kv_ref, out_ref, k_lo, k_hi, v_lo, v_hi):
    scale = head_dim ** -0.5

    @pl.when(pl.program_id(0) == 0)
    def _():
        kv = kv_ref[...].astype(F32)
        low = lax.broadcasted_iota(jnp.int32, kv.shape, 1) < head_dim
        keys = jnp.where(low, kv, 0.0)
        vals = jnp.where(low, 0.0, kv)
        k_lo[...] = keys.astype(BF16)
        k_hi[...] = pltpu.roll(keys, head_dim, 1).astype(BF16)
        v_hi[...] = vals.astype(BF16)
        v_lo[...] = pltpu.roll(vals, head_dim, 1).astype(BF16)

    blk = min(256, seq)
    row = lax.broadcasted_iota(jnp.int32, (blk, blk), 0)
    col = lax.broadcasted_iota(jnp.int32, (blk, blk), 1)
    allowed = col <= row
    for b in range(seq // blk):
        q = q_ref[pl.ds(b * blk, blk), :]
        keys = (b + 1) * blk
        ctx = None
        for k_ref, v_ref in ((k_lo, v_lo), (k_hi, v_hi)):
            s = lax.dot_general(q, k_ref[pl.ds(0, keys), :], (((1,), (1,)), ((), ())), preferred_element_type=F32)
            diag = jnp.where(allowed, s[:, b * blk:], -1e30)
            s = diag if b == 0 else jnp.concatenate([s[:, :b * blk], diag], axis=1)
            e = jnp.exp((s - jnp.max(s, axis=-1, keepdims=True)) * scale)
            p = (e * (1.0 / jnp.sum(e, axis=-1, keepdims=True))).astype(BF16)
            part = jnp.dot(p, v_ref[pl.ds(0, keys), :], preferred_element_type=F32)
            ctx = part if ctx is None else ctx + part
        out_ref[pl.ds(b * blk, blk), :] = ctx.astype(BF16)


def attend(q, kv, head_dim):
    seq, q_cols = q.shape
    flops = 2 * seq * seq * q_cols * 4
    return pl.pallas_call(
        functools.partial(attend_kernel, seq, head_dim),
        grid=(q_cols // LANES,),
        in_specs=[pl.BlockSpec((seq, LANES), lambda h: (0, h)), pl.BlockSpec((seq, LANES), lambda h: (0, 0))],
        out_specs=pl.BlockSpec((seq, LANES), lambda h: (0, h)),
        out_shape=jax.ShapeDtypeStruct((seq, q_cols), BF16),
        scratch_shapes=[pltpu.VMEM((seq, LANES), BF16)] * 4,
        compiler_params=pltpu.CompilerParams(vmem_limit_bytes=VMEM_LIMIT),
        cost_estimate=pl.CostEstimate(flops=flops, bytes_accessed=4 * seq * q_cols, transcendentals=0),
        name="attend",
    )(q, kv)


def contract_kernel(num, final, j0, steps, tn, order, ctx_hbm, act_hbm, wo_hbm, wd_hbm, *refs):
    refs, (ctx_buf, act_buf, sem) = refs[:-3], refs[-3:]
    blk = ctx_hbm.shape[1]
    cps = []
    for k in range(num):
        rows = pl.ds(k * blk, blk)
        cps.append(pltpu.make_async_copy(act_hbm.at[order[k]], act_buf.at[rows], sem))
        cps.append(pltpu.make_async_copy(ctx_hbm.at[order[k]], ctx_buf.at[rows], sem))
    for cp in cps:
        cp.start()

    def product(j, wo, wd):
        @pl.when(j == 0)
        def _():
            for cp in cps:
                cp.wait()

        acc = jnp.dot(act_buf[...], wd[...], preferred_element_type=F32)
        acc = acc + jnp.dot(ctx_buf[...], wo[...], preferred_element_type=F32)
        return acc.reshape(num, blk, tn)

    def pair_body(wo, wd, send):
        send[...] = product(pl.program_id(0), wo, wd).astype(BF16)

    def own_body(wo, wd, add, far_lo, far_hi, up, down, up_lo, down_hi, own):
        j = pl.program_id(0)
        acc = product(j, wo, wd) + add[...].astype(F32)
        own[...] = acc[3]
        up[...] = acc[1].astype(BF16)
        down[...] = acc[2].astype(BF16)

        @pl.when(j < steps // 2)
        def _():
            far_lo[...] = acc[0].astype(BF16)
            up_lo[...] = acc[1]

        @pl.when(j >= steps // 2)
        def _():
            far_hi[...] = acc[0].astype(BF16)
            down_hi[...] = acc[2]

    weights = [pl.BlockSpec((w.shape[0], tn), lambda j: (0, j0 + j)) for w in (wo_hbm, wd_hbm)]
    block = pl.BlockSpec((num, blk, tn), lambda j: (0, 0, j))
    one = pl.BlockSpec((blk, tn), lambda j: (0, j))
    lo = pl.BlockSpec((blk, tn), lambda j: (0, jnp.minimum(j, steps // 2 - 1)))
    hi = pl.BlockSpec((blk, tn), lambda j: (0, jnp.maximum(j - steps // 2, 0)))
    if final:
        pltpu.emit_pipeline(own_body, grid=(steps,), in_specs=weights + [pl.BlockSpec((num, blk, tn), lambda j: (0, 0, final[0] + j))],
                            out_specs=[lo, hi, one, one, lo, hi, one])(wo_hbm, wd_hbm, *refs)
    else:
        pltpu.emit_pipeline(pair_body, grid=(steps,), in_specs=weights, out_specs=[block])(wo_hbm, wd_hbm, *refs)


def contract(order, ctx, act, w_out, w_down, col0, cols, add=None, add_col0=0):
    num = order.shape[0]
    _, blk, _ = ctx.shape
    tn = min(512, cols // 2)
    steps = cols // tn
    any_spec = pl.BlockSpec(memory_space=pl.ANY)
    args = [order, ctx, act, w_out, w_down]
    if add is not None:
        args.append(add)
        half, full = (lambda t: jax.ShapeDtypeStruct((blk, cols // 2), t)), (lambda t: jax.ShapeDtypeStruct((blk, cols), t))
        out_shape = [half(BF16), half(BF16), full(BF16), full(BF16), half(F32), half(F32), full(F32)]
    else:
        out_shape = [jax.ShapeDtypeStruct((num, blk, cols), BF16)]
    depth = w_out.shape[0] + w_down.shape[0]
    return pl.pallas_call(
        functools.partial(contract_kernel, num, None if add is None else (add_col0 // tn,), col0 // tn, steps, tn),
        in_specs=[pl.BlockSpec(memory_space=pltpu.SMEM)] + [any_spec] * (len(args) - 1),
        out_specs=[any_spec] * len(out_shape),
        out_shape=out_shape,
        scratch_shapes=[
            pltpu.VMEM((num * blk, w_out.shape[0]), BF16), pltpu.VMEM((num * blk, w_down.shape[0]), BF16),
            pltpu.SemaphoreType.DMA,
        ],
        compiler_params=pltpu.CompilerParams(vmem_limit_bytes=VMEM_LIMIT),
        cost_estimate=pl.CostEstimate(flops=2 * num * blk * cols * depth, bytes_accessed=2 * depth * cols, transcendentals=0),
        name="contract_pair" if add is None else "contract_own",
    )(*args)


def merge_kernel(up_lo, down_hi, below, above, up_any, down_any, up, down):
    up[...] = (up_lo[...] + below[...].astype(F32)).astype(BF16)
    down[...] = (down_hi[...] + above[...].astype(F32)).astype(BF16)


def merge(up_lo, down_hi, below, above, up, down):
    blk, half = up_lo.shape
    cw = min(1024, half)
    any_spec = pl.BlockSpec(memory_space=pl.ANY)
    part = pl.BlockSpec((blk, cw), lambda j: (0, j))
    return pl.pallas_call(
        merge_kernel,
        grid=(half // cw,),
        in_specs=[part] * 4 + [any_spec] * 2,
        out_specs=[part, pl.BlockSpec((blk, cw), lambda j: (0, half // cw + j))],
        out_shape=[jax.ShapeDtypeStruct(up.shape, BF16)] * 2,
        input_output_aliases={4: 0, 5: 1},
        compiler_params=pltpu.CompilerParams(vmem_limit_bytes=VMEM_LIMIT),
        cost_estimate=pl.CostEstimate(flops=16 * blk * half, bytes_accessed=16 * blk * half, transcendentals=0),
        name="merge",
    )(up_lo, down_hi, below, above, up, down)


def finish_kernel(x, own, below, above, *refs):
    y = refs[-1]
    total = own[...] + (below[...].astype(F32) + above[...].astype(F32))
    y[...] = (x[...].astype(F32) + total).astype(BF16)


def finish(hidden, batch_id, col0, own, below, above, result):
    blk, cols = own.shape
    cw = min(1024, cols)
    j0 = col0 // cw
    part = pl.BlockSpec((blk, cw), lambda j: (0, j))
    wide = pl.BlockSpec((None, blk, cw), lambda j: (batch_id, 0, j0 + j))
    args, in_specs, aliases = [hidden, own, below, above], [wide, part, part, part], {}
    if result is not None:
        args.append(result)
        in_specs.append(pl.BlockSpec(memory_space=pl.ANY))
        aliases = {4: 0}
    return pl.pallas_call(
        finish_kernel,
        grid=(cols // cw,),
        in_specs=in_specs,
        out_specs=wide,
        out_shape=jax.ShapeDtypeStruct(hidden.shape, BF16),
        input_output_aliases=aliases,
        compiler_params=pltpu.CompilerParams(vmem_limit_bytes=VMEM_LIMIT),
        cost_estimate=pl.CostEstimate(flops=16 * blk * cols, bytes_accessed=12 * blk * cols, transcendentals=0),
        name="finish",
    )(*args)


def solution(mesh):
    tp = mesh.shape["tp"]
    chips = tp // 2
    assert tp == 2 * chips and chips == 4
    pair = [(i, i ^ 1) for i in range(tp)]
    up_ring = [(i, (i + 2) % tp) for i in range(tp)]
    down_ring = [(i, (i - 2) % tp) for i in range(tp)]

    def layer(hidden_blk, attn_gain, attn_bias, mlp_gain, mlp_bias, w_qkv_part, w_out_part, w_up_part, w_down_part, positions):
        batch, seq_rows, width = hidden_blk.shape
        seq = seq_rows * tp
        w_qkv = w_qkv_part.reshape(width, w_qkv_part.shape[2])
        q_cols = w_out_part.shape[0]
        head_dim = (w_qkv.shape[1] - q_cols) // 2
        norms = [v.reshape(1, width) for v in (attn_gain, attn_bias, mlp_gain, mlp_bias)]
        tabs = [t.reshape(tp, seq_rows, LANES) for t in rotary_tables(positions, head_dim)]

        parts = []
        for b in range(batch):
            cut = [(0, seq_rows // 2), (seq_rows // 2, seq_rows)] if b == 0 else [(0, seq_rows)]
            parts += [(b, lo, hi) for lo, hi in cut]
        gathered = [lax.all_gather(hidden_blk[b, lo:hi], "tp", axis=0, tiled=False) for b, lo, hi in parts]

        last_done, result = [positions], [None]

        def in_turn(first):
            out = lax.optimization_barrier((first, last_done[0]))
            if last_done[0] is result:
                result[0] = out[1][0]
            return out[0]

        x32 = hidden_blk.astype(F32)
        mean = jnp.mean(x32, axis=-1, keepdims=True)
        centered = x32 - mean
        rstd = lax.rsqrt(jnp.mean(centered * centered, axis=-1, keepdims=True) + 1e-5)
        stats = lax.all_gather(jnp.stack([mean[..., 0], rstd[..., 0]]), "tp", axis=2, tiled=False)
        stats = jnp.broadcast_to(stats[..., None], (2, batch, tp, seq_rows, LANES))

        expanded = [None] * batch

        def run_expand(b):
            for (pb, lo, hi), xg in zip(parts, gathered):
                if pb == b:
                    expanded[b] = expand(in_turn(xg), b, lo, seq_rows, stats, norms, w_qkv, w_up_part, tabs, expanded[b])
                    last_done[0] = expanded[b][1]

        me = lax.axis_index("tp")
        chip, core = me // 2, me % 2
        targets = jnp.stack([(chip + 2) % chips, (chip + 1) % chips, (chip + chips - 1) % chips, chip]).astype(jnp.int32)
        own_order = targets * 2 + core
        pair_order = targets * 2 + (1 - core)
        ring_up = lambda v: lax.ppermute(v, "tp", up_ring)
        ring_down = lambda v: lax.ppermute(v, "tp", down_ring)

        ctxs, arrived, started, merged = {}, {}, {}, {}

        def run_attend(b):
            q, kv, _ = expanded[b]
            q = in_turn(q)
            ctx = attend(q.reshape(seq, q_cols), kv.reshape(seq, LANES), head_dim)
            last_done[0] = ctx
            ctxs[b] = ctx.reshape(tp, seq_rows, q_cols)

        def run_pair(span):
            b, c, w = span
            (send,) = contract(in_turn(pair_order), ctxs[b], expanded[b][2], w_out_part, w_down_part, c, w)
            last_done[0] = send
            arrived[span] = lax.ppermute(send, "tp", pair)

        def run_own(span):
            b, c, w = span
            pb, pc, pw = next(p for p in arrived if p[0] == b and p[1] <= c and c + w <= p[1] + p[2])
            far_lo, far_hi, up, down, up_lo, down_hi, own = contract(
                in_turn(own_order), ctxs[b], expanded[b][2], w_out_part, w_down_part, c, w, arrived[pb, pc, pw], c - pc)
            last_done[0] = far_lo
            started[span] = (up_lo, down_hi, ring_up(far_lo), ring_down(far_hi), up, down, own)

        def run_merge(span):
            up_lo, down_hi, below, above, up, down, own = started[span]
            up, down = merge(in_turn(up_lo), down_hi, below, above, up, down)
            last_done[0] = up
            merged[span] = (own, ring_up(up), ring_down(down))

        def run_finish(span):
            own, below, above = merged[span]
            result[0] = finish(hidden_blk, span[0], span[1], in_turn(own), below, above, result[0])
            last_done[0] = result

        whole = [(b, 0, width) for b in range(batch)]
        last, half, quarter = batch - 1, width // 2, width // 4
        pairs = [(last, 0, half), (last, half, half)]
        ends = [(last, 0, half), (last, half, quarter), (last, half + quarter, quarter)]
        run_expand(0)
        run_attend(0)
        run_pair(whole[0])
        for b in range(1, batch):
            run_expand(b)
            if b >= 2:
                run_finish(whole[b - 2])
            run_own(whole[b - 1])
            run_attend(b)
            if b < last:
                run_pair(whole[b])
            run_merge(whole[b - 1])
        run_pair(pairs[0])
        run_pair(pairs[1])
        run_own(ends[0])
        run_finish(whole[last - 1])
        run_own(ends[1])
        run_merge(ends[0])
        run_own(ends[2])
        run_merge(ends[1])
        run_finish(ends[0])
        run_merge(ends[2])
        run_finish(ends[1])
        run_finish(ends[2])
        return result[0]

    return jax.shard_map(
        layer, mesh=mesh,
        in_specs=(P("dp", "tp", None), P(), P(), P(), P(), P(None, "tp", None), P("tp", None), P(None, "tp"), P("tp", None), P()),
        out_specs=P("dp", "tp", None), check_vma=False)
```

time: 1100 us -> 1010 us (0.918)
  waiting for transfers between devices: 118 us -> 37.2 us
  other arithmetic: 48.6 us -> 14.2 us
  blocking collectives: 0 us -> 20.5 us
    ppermute x35 -> x24, waiting for transfers between devices: 79.2 us -> 27.8 us  [the longest x10 27.8 us: layer(): ring_up = lambda v: lax.ppermute(v, 'tp', up_ring)]
    all_gather x4, waiting for transfers between devices: 37.2 us -> 7.98 us  [layer(): lax.all_gather(hidden_blk[b, lo:hi], 'tp', axis=0, tiled=False)]
    dynamic_update_slice x9 -> x0, other arithmetic: 23.6 us -> none  [run_finish(): result[0] = lax.dynamic_update_slice(result[0], rows[None], (b, 0, c + lo))]
    all_gather x0 -> x1, blocking collectives: none -> 20.5 us  [layer(): lax.all_gather(jnp.stack([mean[..., 0], rstd[..., 0]]), 'tp', axis=2, til...]
    pallas_call x10 -> x19, Pallas kernels: 358 us -> 376 us  [the longest x9 335 us: contract(): pl.pallas_call(functools.partial(contract_kernel, num, None if add is Non...]
    convert_element_type x10 -> x0, other arithmetic: 16.6 us -> none  [the longest x5 9.23 us: run_merge(): up_lo = (up_lo + from_below.astype(F32)).astype(BF16)]
    ppermute x35 -> x24, starting transfers between devices: 36.4 us -> 32.8 us  [the longest x10 30.4 us: layer(): ring_down = lambda v: lax.ppermute(v, 'tp', down_ring)]
  transfers between devices with their start and end apart: 39 -> 28, of which waited for: 9 -> 5; matrix products, arithmetic and copies ran while one was open for 5% -> 2% of each run, Pallas kernels for 49% -> 78%
where the time goes in v2:
time: 1010 us; the launch traced here: 1000 us
  Pallas kernels  874 us (87%)
  waiting for transfers between devices  37.2 us (4%)
  starting transfers between devices  33 us (3%)
  blocking collectives  20.5 us (2%)
  other arithmetic  14.2 us (1%)
  between operations  14 us (1%)
  local copies, waits for them, and re-layouts  10.6 us (1%)
    pallas_call x4, Pallas kernels, expand(): pl.pallas_call(functools.partial(expand_kernel, devs, width, q_tiles, up_...  417 us
    pallas_call x9, Pallas kernels, contract(): pl.pallas_call(functools.partial(contract_kernel, num, None if add is Non...  335 us
    pallas_call x3, Pallas kernels, attend(): pl.pallas_call(functools.partial(attend_kernel, seq, head_dim), grid=(q_c...  81.8 us
    ppermute x10, starting transfers between devices, layer(): ring_down = lambda v: lax.ppermute(v, 'tp', down_ring)  30.4 us
    ppermute x10, waiting for transfers between devices, layer(): ring_up = lambda v: lax.ppermute(v, 'tp', up_ring)  27.8 us
    pallas_call x5, Pallas kernels, finish(): pl.pallas_call(finish_kernel, grid=(cols // cw,), in_specs=in_specs, out_...  24.3 us
    all_gather x1, blocking collectives, layer(): lax.all_gather(jnp.stack([mean[..., 0], rstd[..., 0]]), 'tp', axis=2, til...  20.5 us
  transfers between devices with their start and end apart: 28, of which 5 were waited for; matrix products, arithmetic and copies ran while one was open for 2% of the time, Pallas kernels for 78%

profile of v2, /device:TPU:112, one launch (start us, length us, event | category | flops | bytes accessed | tf_op | source)
XLA Modules:
  0.0 1003.9 jit_solution(7078730709760585652)
XLA Ops:
  6.6 3.1 fusion.7
  9.8 0.7 all-gather.8.cloned.1.call-update
  10.6 4.6 fusion.6
  15.3 0.6 all-gather.12.cloned.1.call-update
  16.0 4.3 convert_reduce_fusion
  20.3 4.7 fusion.1
  25.0 20.5 %all-gather = f32[2,3,1024]{2,0,1:T(2,128)S(1)} all-gather(f32[2,3,128]{2,0,1:T(2,128)S(1)} %pad_maximum_fusion.4), channel_id=2, replica_groups=mesh['dp'=2,'tp'=8] {'tp'}, dimensions={2}, use_global_device_ids=true | all-gather | bytes 27648 | tf_op jit(solution)/shard_map/all_gather | solution.py:408
  45.6 0.1 pad.5.clone
  45.7 0.1 pad.2.clone
  45.7 1.9 fusion.4
  47.7 0.7 broadcast_add_fusion
  48.3 2.2 fusion.2
  50.5 7.9 all-gather.10.cloned.1.call-done.x_hbm
  58.4 2.7 broadcast_in_dim.6.mean_ref.rstd_ref
  61.0 72.2 %expand.4 = (bf16[8,128,1024]{2,1,0:T(8,128)(2,1)}, bf16[8,128,128]{2,1,0:T(8,128)(2,1)}, bf16[8,128,4096]{2,1,0:T(8,128)(2,1)}) custom-call(bf16[8,64,8192]{2,1,0:T(8,128)(2,1)} %all-gather.10.cloned.1.call-done.x_hbm, f32[2,3,8,128,128]{4,3,2,1,0:T(8,128)} %broadcast_in_dim.6.mean_ref.rstd_ref, f32[2,3,8,128,128]{4,3,2,1,0:T(8,128)} %broadcast_in_dim.6.mean_ref.rstd_ref, ...), custom_call_target="tpu_custom_call" | custom-call | flops 44023414784 | bytes 83886080 | tf_op jit(solution)/shard_map/expand/pallas_call | solution.py:172
  133.3 71.6 %expand.5 = (bf16[8,128,1024]{2,1,0:T(8,128)(2,1)}, bf16[8,128,128]{2,1,0:T(8,128)(2,1)}, bf16[8,128,4096]{2,1,0:T(8,128)(2,1)}) custom-call(bf16[8,64,8192]{2,1,0:T(8,128)(2,1)} %all-gather.8.cloned.1.call-done.x_hbm, f32[2,3,8,128,128]{4,3,2,1,0:T(8,128)} %broadcast_in_dim.6.mean_ref.rstd_ref, ...), custom_call_target="tpu_custom_call", output_to_operand_aliasing={{0}: (14, {}), {1}: (15, {}), {2}: (16, {})} | custom-call | flops 44023414784 | bytes 83886080 | tf_op jit(solution)/shard_map/expand/pallas_call | solution.py:172
  204.8 27.1 %attend.3 = bf16[1024,1024]{1,0:T(8,128)(2,1)} custom-call(bf16[1024,1024]{1,0:T(8,128)(2,1)} %bitcast.59, bf16[1024,128]{1,0:T(8,128)(2,1)} %bitcast.62), custom_call_target="tpu_custom_call" | custom-call | flops 8589934592 | bytes 4194304 | tf_op jit(solution)/shard_map/attend/pallas_call | solution.py:225
  232.0 52.1 %contract_pair.4 = bf16[4,128,8192]{2,1,0:T(8,128)(2,1)} custom-call(s32[4]{0:T(128)} %get-tuple-element.135.order, bf16[8,128,1024]{2,1,0:T(8,128)(2,1)} %bitcast.56, bf16[8,128,4096]{2,1,0:T(8,128)(2,1)} %get-tuple-element.101.act_hbm, bf16[1024,8192]{1,0:T(8,128)(2,1)} %wo_hbm.17, bf16[4096,8192]{1,0:T(8,128)(2,1)} %wd_hbm.17), custom_call_target="tpu_custom_call" | custom-call | flops 42949672960 | bytes 83886080 | tf_op jit(solution)/shard_map/contract_pair/pallas_call | solution.py:305
  284.0 0.7 collective-permute-start
  284.7 0.5 broadcast_add_fusion.1.order
  285.2 136.7 %expand.6 = (bf16[8,128,1024]{2,1,0:T(8,128)(2,1)}, bf16[8,128,128]{2,1,0:T(8,128)(2,1)}, bf16[8,128,4096]{2,1,0:T(8,128)(2,1)}) custom-call(bf16[8,128,8192]{2,1,0:T(8,128)(2,1)} %all-gather.6.cloned.1.call-done.x_hbm, f32[2,3,8,128,128]{4,3,2,1,0:T(8,128)} %broadcast_in_dim.6.mean_ref.rstd_ref, f32[2,3,8,128,128]{4,3,2,1,0:T(8,128)} %broadcast_in_dim.6.mean_ref.rstd_ref, ...), custom_call_target="tpu_custom_call" | custom-call | flops 88046829568 | bytes 83886080 | tf_op jit(solution)/shard_map/expand/pallas_call | solution.py:172
  422.0 53.8 %contract_own.5 = (bf16[128,4096]{1,0:T(8,128)(2,1)}, bf16[128,4096]{1,0:T(8,128)(2,1)}, bf16[128,8192]{1,0:T(8,128)(2,1)}, bf16[128,8192]{1,0:T(8,128)(2,1)}, f...) custom-call(s32[4]{0:T(128)} %broadcast_add_fusion.1.order, bf16[8,128,1024]{2,1,0:T(8,128)(2,1)} %bitcast.57, ...), custom_call_target="tpu_custom_call" | custom-call | flops 42949672960 | bytes 83886080 | tf_op jit(solution)/shard_map/contract_own/pallas_call | solution.py:305
  475.8 0.6 collective-permute-start.1
  476.4 27.3 %attend.4 = bf16[1024,1024]{1,0:T(8,128)(2,1)} custom-call(bf16[1024,1024]{1,0:T(8,128)(2,1)} %bitcast.58, bf16[1024,128]{1,0:T(8,128)(2,1)} %bitcast.61), custom_call_target="tpu_custom_call" | custom-call | flops 8589934592 | bytes 4194304 | tf_op jit(solution)/shard_map/attend/pallas_call | solution.py:225
  503.7 2.7 collective-permute-start.2
  506.4 52.1 %contract_pair.5 = bf16[4,128,8192]{2,1,0:T(8,128)(2,1)} custom-call(s32[4]{0:T(128)} %get-tuple-element.135.order, bf16[8,128,1024]{2,1,0:T(8,128)(2,1)} %bitcast.53, bf16[8,128,4096]{2,1,0:T(8,128)(2,1)} %get-tuple-element.111.act_hbm, bf16[1024,8192]{1,0:T(8,128)(2,1)} %wo_hbm.17, bf16[4096,8192]{1,0:T(8,128)(2,1)} %wd_hbm.17), custom_call_target="tpu_custom_call" | custom-call | flops 42949672960 | bytes 83886080 | tf_op jit(solution)/shard_map/contract_pair/pallas_call | solution.py:305
  558.5 0.1 collective-permute-start.5
  558.6 4.6 merge.5
  563.3 3.2 collective-permute-start.4
  566.5 136.3 %expand.7 = (bf16[8,128,1024]{2,1,0:T(8,128)(2,1)}, bf16[8,128,128]{2,1,0:T(8,128)(2,1)}, bf16[8,128,4096]{2,1,0:T(8,128)(2,1)}) custom-call(bf16[8,128,8192]{2,1,0:T(8,128)(2,1)} %all-gather.12.cloned.1.call-done.x_hbm, f32[2,3,8,128,128]{4,3,2,1,0:T(8,128)} %broadcast_in_dim.6.mean_ref.rstd_ref, f32[2,3,8,128,128]{4,3,2,1,0:T(8,128)} %broadcast_in_dim.6.mean_ref.rstd_ref, ...), custom_call_target="tpu_custom_call" | custom-call | flops 88046829568 | bytes 83886080 | tf_op jit(solution)/shard_map/expand/pallas_call | solution.py:172
  702.8 7.5 finish.5.refs_0_
  710.3 53.8 %contract_own.6 = (bf16[128,4096]{1,0:T(8,128)(2,1)}, bf16[128,4096]{1,0:T(8,128)(2,1)}, bf16[128,8192]{1,0:T(8,128)(2,1)}, bf16[128,8192]{1,0:T(8,128)(2,1)}, f...) custom-call(s32[4]{0:T(128)} %broadcast_add_fusion.1.order, bf16[8,128,1024]{2,1,0:T(8,128)(2,1)} %bitcast.54, ...), custom_call_target="tpu_custom_call" | custom-call | flops 42949672960 | bytes 83886080 | tf_op jit(solution)/shard_map/contract_own/pallas_call | solution.py:305
  764.1 0.1 collective-permute-start.6
  764.2 3.2 collective-permute-start.7
  767.4 27.4 %attend.5 = bf16[1024,1024]{1,0:T(8,128)(2,1)} custom-call(bf16[1024,1024]{1,0:T(8,128)(2,1)} %bitcast.55, bf16[1024,128]{1,0:T(8,128)(2,1)} %bitcast.60), custom_call_target="tpu_custom_call" | custom-call | flops 8589934592 | bytes 4194304 | tf_op jit(solution)/shard_map/attend/pallas_call | solution.py:225
  794.8 4.6 merge.6
  799.5 28.8 %contract_pair.6 = bf16[4,128,4096]{2,1,0:T(8,128)(2,1)} custom-call(s32[4]{0:T(128)} %get-tuple-element.135.order, bf16[8,128,1024]{2,1,0:T(8,128)(2,1)} %bitcast.24, bf16[8,128,4096]{2,1,0:T(8,128)(2,1)} %get-tuple-element.134.act_hbm, bf16[1024,8192]{1,0:T(8,128)(2,1)} %wo_hbm.17, bf16[4096,8192]{1,0:T(8,128)(2,1)} %wd_hbm.17), custom_call_target="tpu_custom_call" | custom-call | flops 21474836480 | bytes 41943040 | tf_op jit(solution)/shard_map/contract_pair/pallas_call | solution.py:305
  828.3 0.1 collective-permute-start.8
  828.4 28.8 %contract_pair.7 = bf16[4,128,4096]{2,1,0:T(8,128)(2,1)} custom-call(s32[4]{0:T(128)} %get-tuple-element.135.order, bf16[8,128,1024]{2,1,0:T(8,128)(2,1)} %bitcast.25, bf16[8,128,4096]{2,1,0:T(8,128)(2,1)} %get-tuple-element.134.act_hbm, bf16[1024,8192]{1,0:T(8,128)(2,1)} %wo_hbm.17, bf16[4096,8192]{1,0:T(8,128)(2,1)} %wd_hbm.17), custom_call_target="tpu_custom_call" | custom-call | flops 21474836480 | bytes 41943040 | tf_op jit(solution)/shard_map/contract_pair/pallas_call | solution.py:305
  857.2 0.5 collective-permute-start.11
  857.8 3.2 collective-permute-start.10
  861.0 29.9 %contract_own.7 = (bf16[128,2048]{1,0:T(8,128)(2,1)}, bf16[128,2048]{1,0:T(8,128)(2,1)}, bf16[128,4096]{1,0:T(8,128)(2,1)}, bf16[128,4096]{1,0:T(8,128)(2,1)}, f...) custom-call(s32[4]{0:T(128)} %broadcast_add_fusion.1.order, bf16[8,128,1024]{2,1,0:T(8,128)(2,1)} %bitcast.26, ...), custom_call_target="tpu_custom_call" | custom-call | flops 21474836480 | bytes 41943040 | tf_op jit(solution)/shard_map/contract_own/pallas_call | solution.py:305
  890.9 0.1 collective-permute-start.12
  891.0 16.8 %collective-permute-done.9.below = bf16[128,8192]{1,0:T(8,128)(2,1)} collective-permute-done((bf16[128,8192]{1,0:T(8,128)(2,1)}, bf16[128,8192]{1,0:T(8,128)(2,1)}, u32[]{:S(2)}, u32[]{:S(2)}) %collective-permute-start.9) | collective-permute-done | bytes 2097184 | tf_op jit(solution)/shard_map/ppermute | solution.py:424
  907.8 7.5 finish.6.refs_0_
  915.3 2.1 collective-permute-start.13
  917.4 17.9 %contract_own.8 = (bf16[128,1024]{1,0:T(8,128)(2,1)}, bf16[128,1024]{1,0:T(8,128)(2,1)}, bf16[128,2048]{1,0:T(8,128)(2,1)}, bf16[128,2048]{1,0:T(8,128)(2,1)}, f...) custom-call(s32[4]{0:T(128)} %broadcast_add_fusion.1.order, bf16[8,128,1024]{2,1,0:T(8,128)(2,1)} %bitcast.27, ...), custom_call_target="tpu_custom_call" | custom-call | flops 10737418240 | bytes 20971520 | tf_op jit(solution)/shard_map/contract_own/pallas_call | solution.py:305
  935.3 0.1 collective-permute-start.14
  935.4 3.2 collective-permute-start.15
  938.6 2.8 merge.7
  941.4 3.2 collective-permute-start.17
  944.6 17.9 %contract_own.9 = (bf16[128,1024]{1,0:T(8,128)(2,1)}, bf16[128,1024]{1,0:T(8,128)(2,1)}, bf16[128,2048]{1,0:T(8,128)(2,1)}, bf16[128,2048]{1,0:T(8,128)(2,1)}, f...) custom-call(s32[4]{0:T(128)} %broadcast_add_fusion.1.order, bf16[8,128,1024]{2,1,0:T(8,128)(2,1)} %bitcast.28, ...), custom_call_target="tpu_custom_call" | custom-call | flops 10737418240 | bytes 20971520 | tf_op jit(solution)/shard_map/contract_own/pallas_call | solution.py:305
  962.5 0.1 collective-permute-start.18
  962.7 3.2 collective-permute-start.19
  965.9 2.2 merge.8
  968.1 0.2 collective-permute-done.16.below
  968.3 3.1 collective-permute-start.21
  971.4 4.3 finish.7.refs_0_
  975.6 2.2 merge.9
  977.9 3.2 collective-permute-start.23
  981.1 4.0 collective-permute-done.20.below
  985.1 2.5 finish.8.refs_0_
  987.6 6.8 collective-permute-done.22.below
  994.4 2.5 finish.9
  (47 shorter events, 0.5 us)
Async XLA Ops:
  6.5 51.8 %all-gather.10.cloned.1.call-start = ((), (), s32[]{:S(2)}) async-start(), calls=%async_computation.2 | async-start | bytes 9437184 | tf_op jit(solution)/shard_map/all_gather | solution.py:394
  9.7 123.6 %all-gather.8.cloned.1.call-start = ((), (), s32[]{:S(2)}) async-start(), calls=%async_computation.1 | async-start | bytes 9437184 | tf_op jit(solution)/shard_map/all_gather | solution.py:394
  10.5 274.7 %all-gather.6.cloned.1.call-start = ((), (), s32[]{:S(2)}) async-start(), calls=%async_computation | async-start | bytes 18874368 | tf_op jit(solution)/shard_map/all_gather | solution.py:394
  15.3 548.0 %all-gather.12.cloned.1.call-start = ((), (), s32[]{:S(2)}) async-start(), calls=%async_computation.3 | async-start | bytes 18874368 | tf_op jit(solution)/shard_map/all_gather | solution.py:394
  20.3 25.3 %copy-start = (s32[1024]{0:T(1024)S(1)}, s32[1024]{0:T(1024)}, u32[]{:S(2)}) copy-start(s32[1024]{0:T(1024)} %param.19) | copy-start | bytes 12292
  284.0 137.9 %collective-permute-start = (bf16[4,128,8192]{2,1,0:T(8,128)(2,1)}, bf16[4,128,8192]{2,1,0:T(8,128)(2,1)}, u32[]{:S(2)}, u32[]{:S(2)}) collective-permute-start(bf16[4,128,8192]{2,1,0:T(8,128)(2,1)} %contract_pair.4), channel_id=1, source_target_pairs={{0,1},{1,0},{2,3},{3,2},{4,5},{5,4},{6,7},{7,6},{8,9},{9,8},{10,11... | collective-permute-start | bytes 25165832 | tf_op jit(solution)/shard_map/ppermute | solution.py:440
  475.8 82.8 %collective-permute-start.1 = (bf16[128,4096]{1,0:T(8,128)(2,1)}, bf16[128,4096]{1,0:T(8,128)(2,1)}, u32[]{:S(2)}, u32[]{:S(2)}) collective-permute-start(bf16[128,4096]{1,0:T(8,128)(2,1)} %get-tuple-element.108), channel_id=1, source_target_pairs={{0,2},{1,3},{2,4},{3,5},{4,6},{5,7},{6,0},{7,1},{8,10},{9,11},{10,... | collective-permute-start | bytes 3145736 | tf_op jit(solution)/shard_map/ppermute | solution.py:424
  503.7 54.9 %collective-permute-start.2 = (bf16[128,4096]{1,0:T(8,128)(2,1)}, bf16[128,4096]{1,0:T(8,128)(2,1)}, u32[]{:S(2)}, u32[]{:S(2)}) collective-permute-start(bf16[128,4096]{1,0:T(8,128)(2,1)} %get-tuple-element.114), channel_id=1, source_target_pairs={{0,6},{1,7},{2,0},{3,1},{4,2},{5,3},{6,4},{7,5},{8,14},{9,15},{10,... | collective-permute-start | bytes 3145736 | tf_op jit(solution)/shard_map/ppermute | solution.py:425
  558.5 151.8 %collective-permute-start.5 = (bf16[4,128,8192]{2,1,0:T(8,128)(2,1)}, bf16[4,128,8192]{2,1,0:T(8,128)(2,1)}, u32[]{:S(2)}, u32[]{:S(2)}) collective-permute-start(bf16[4,128,8192]{2,1,0:T(8,128)(2,1)} %contract_pair.5), channel_id=1, source_target_pairs={{0,1},{1,0},{2,3},{3,2},{4,5},{5,4},{6,7},{7,6},{8,9},{9,8},{10,11... | collective-permute-start | bytes 25165832 | tf_op jit(solution)/shard_map/ppermute | solution.py:440
  563.2 139.5 %collective-permute-start.3 = (bf16[128,8192]{1,0:T(8,128)(2,1)}, bf16[128,8192]{1,0:T(8,128)(2,1)}, u32[]{:S(2)}, u32[]{:S(2)}) collective-permute-start(bf16[128,8192]{1,0:T(8,128)(2,1)} %get-tuple-element.117), channel_id=1, source_target_pairs={{0,2},{1,3},{2,4},{3,5},{4,6},{5,7},{6,0},{7,1},{8,10},{9,11},{10,... | collective-permute-start | bytes 6291464 | tf_op jit(solution)/shard_map/ppermute | solution.py:424
  563.3 139.5 %collective-permute-start.4 = (bf16[128,8192]{1,0:T(8,128)(2,1)}, bf16[128,8192]{1,0:T(8,128)(2,1)}, u32[]{:S(2)}, u32[]{:S(2)}) collective-permute-start(bf16[128,8192]{1,0:T(8,128)(2,1)} %get-tuple-element.121), channel_id=1, source_target_pairs={{0,6},{1,7},{2,0},{3,1},{4,2},{5,3},{6,4},{7,5},{8,14},{9,15},{10,... | collective-permute-start | bytes 6291464 | tf_op jit(solution)/shard_map/ppermute | solution.py:425
  764.1 30.7 %collective-permute-start.6 = (bf16[128,4096]{1,0:T(8,128)(2,1)}, bf16[128,4096]{1,0:T(8,128)(2,1)}, u32[]{:S(2)}, u32[]{:S(2)}) collective-permute-start(bf16[128,4096]{1,0:T(8,128)(2,1)} %get-tuple-element.125), channel_id=1, source_target_pairs={{0,2},{1,3},{2,4},{3,5},{4,6},{5,7},{6,0},{7,1},{8,10},{9,11},{10,... | collective-permute-start | bytes 3145736 | tf_op jit(solution)/shard_map/ppermute | solution.py:424
  764.2 30.6 %collective-permute-start.7 = (bf16[128,4096]{1,0:T(8,128)(2,1)}, bf16[128,4096]{1,0:T(8,128)(2,1)}, u32[]{:S(2)}, u32[]{:S(2)}) collective-permute-start(bf16[128,4096]{1,0:T(8,128)(2,1)} %get-tuple-element.129), channel_id=1, source_target_pairs={{0,6},{1,7},{2,0},{3,1},{4,2},{5,3},{6,4},{7,5},{8,14},{9,15},{10,... | collective-permute-start | bytes 3145736 | tf_op jit(solution)/shard_map/ppermute | solution.py:425
  828.3 32.7 %collective-permute-start.8 = (bf16[4,128,4096]{2,1,0:T(8,128)(2,1)}, bf16[4,128,4096]{2,1,0:T(8,128)(2,1)}, u32[]{:S(2)}, u32[]{:S(2)}) collective-permute-start(bf16[4,128,4096]{2,1,0:T(8,128)(2,1)} %contract_pair.6), channel_id=1, source_target_pairs={{0,1},{1,0},{2,3},{3,2},{4,5},{5,4},{6,7},{7,6},{8,9},{9,8},{10,11... | collective-permute-start | bytes 12582920 | tf_op jit(solution)/shard_map/ppermute | solution.py:440
  857.2 60.2 %collective-permute-start.11 = (bf16[4,128,4096]{2,1,0:T(8,128)(2,1)}, bf16[4,128,4096]{2,1,0:T(8,128)(2,1)}, u32[]{:S(2)}, u32[]{:S(2)}) collective-permute-start(bf16[4,128,4096]{2,1,0:T(8,128)(2,1)} %contract_pair.7), channel_id=1, source_target_pairs={{0,1},{1,0},{2,3},{3,2},{4,5},{5,4},{6,7},{7,6},{8,9},{9,8},{10,11... | collective-permute-start | bytes 12582920 | tf_op jit(solution)/shard_map/ppermute | solution.py:440
  857.8 50.0 %collective-permute-start.9 = (bf16[128,8192]{1,0:T(8,128)(2,1)}, bf16[128,8192]{1,0:T(8,128)(2,1)}, u32[]{:S(2)}, u32[]{:S(2)}) collective-permute-start(bf16[128,8192]{1,0:T(8,128)(2,1)} %get-tuple-element.132), channel_id=1, source_target_pairs={{0,2},{1,3},{2,4},{3,5},{4,6},{5,7},{6,0},{7,1},{8,10},{9,11},{10,... | collective-permute-start | bytes 6291464 | tf_op jit(solution)/shard_map/ppermute | solution.py:424
  857.8 50.0 %collective-permute-start.10 = (bf16[128,8192]{1,0:T(8,128)(2,1)}, bf16[128,8192]{1,0:T(8,128)(2,1)}, u32[]{:S(2)}, u32[]{:S(2)}) collective-permute-start(bf16[128,8192]{1,0:T(8,128)(2,1)} %get-tuple-element.141), channel_id=1, source_target_pairs={{0,6},{1,7},{2,0},{3,1},{4,2},{5,3},{6,4},{7,5},{8,14},{9,15},{10,... | collective-permute-start | bytes 6291464 | tf_op jit(solution)/shard_map/ppermute | solution.py:425
  890.9 47.8 %collective-permute-start.12 = (bf16[128,2048]{1,0:T(8,128)(2,1)}, bf16[128,2048]{1,0:T(8,128)(2,1)}, u32[]{:S(2)}, u32[]{:S(2)}) collective-permute-start(bf16[128,2048]{1,0:T(8,128)(2,1)} %get-tuple-element.139), channel_id=1, source_target_pairs={{0,2},{1,3},{2,4},{3,5},{4,6},{5,7},{6,0},{7,1},{8,10},{9,11},{10,... | collective-permute-start | bytes 1572872 | tf_op jit(solution)/shard_map/ppermute | solution.py:424
  915.3 23.3 %collective-permute-start.13 = (bf16[128,2048]{1,0:T(8,128)(2,1)}, bf16[128,2048]{1,0:T(8,128)(2,1)}, u32[]{:S(2)}, u32[]{:S(2)}) collective-permute-start(bf16[128,2048]{1,0:T(8,128)(2,1)} %get-tuple-element.147), channel_id=1, source_target_pairs={{0,6},{1,7},{2,0},{3,1},{4,2},{5,3},{6,4},{7,5},{8,14},{9,15},{10,... | collective-permute-start | bytes 1572872 | tf_op jit(solution)/shard_map/ppermute | solution.py:425
  935.3 27.3 %collective-permute-start.14 = (bf16[128,1024]{1,0:T(8,128)(2,1)}, bf16[128,1024]{1,0:T(8,128)(2,1)}, u32[]{:S(2)}, u32[]{:S(2)}) collective-permute-start(bf16[128,1024]{1,0:T(8,128)(2,1)} %get-tuple-element.144), channel_id=1, source_target_pairs={{0,2},{1,3},{2,4},{3,5},{4,6},{5,7},{6,0},{7,1},{8,10},{9,11},{10,... | collective-permute-start | bytes 786440 | tf_op jit(solution)/shard_map/ppermute | solution.py:424
  935.4 30.4 %collective-permute-start.15 = (bf16[128,1024]{1,0:T(8,128)(2,1)}, bf16[128,1024]{1,0:T(8,128)(2,1)}, u32[]{:S(2)}, u32[]{:S(2)}) collective-permute-start(bf16[128,1024]{1,0:T(8,128)(2,1)} %get-tuple-element.160), channel_id=1, source_target_pairs={{0,6},{1,7},{2,0},{3,1},{4,2},{5,3},{6,4},{7,5},{8,14},{9,15},{10,... | collective-permute-start | bytes 786440 | tf_op jit(solution)/shard_map/ppermute | solution.py:425
  941.4 26.9 %collective-permute-start.16 = (bf16[128,4096]{1,0:T(8,128)(2,1)}, bf16[128,4096]{1,0:T(8,128)(2,1)}, u32[]{:S(2)}, u32[]{:S(2)}) collective-permute-start(bf16[128,4096]{1,0:T(8,128)(2,1)} %get-tuple-element.150), channel_id=1, source_target_pairs={{0,2},{1,3},{2,4},{3,5},{4,6},{5,7},{6,0},{7,1},{8,10},{9,11},{10,... | collective-permute-start | bytes 3145736 | tf_op jit(solution)/shard_map/ppermute | solution.py:424
  941.4 30.0 %collective-permute-start.17 = (bf16[128,4096]{1,0:T(8,128)(2,1)}, bf16[128,4096]{1,0:T(8,128)(2,1)}, u32[]{:S(2)}, u32[]{:S(2)}) collective-permute-start(bf16[128,4096]{1,0:T(8,128)(2,1)} %get-tuple-element.165), channel_id=1, source_target_pairs={{0,6},{1,7},{2,0},{3,1},{4,2},{5,3},{6,4},{7,5},{8,14},{9,15},{10,... | collective-permute-start | bytes 3145736 | tf_op jit(solution)/shard_map/ppermute | solution.py:425
  962.5 13.1 %collective-permute-start.18 = (bf16[128,1024]{1,0:T(8,128)(2,1)}, bf16[128,1024]{1,0:T(8,128)(2,1)}, u32[]{:S(2)}, u32[]{:S(2)}) collective-permute-start(bf16[128,1024]{1,0:T(8,128)(2,1)} %get-tuple-element.157), channel_id=1, source_target_pairs={{0,2},{1,3},{2,4},{3,5},{4,6},{5,7},{6,0},{7,1},{8,10},{9,11},{10,... | collective-permute-start | bytes 786440 | tf_op jit(solution)/shard_map/ppermute | solution.py:424
  962.7 13.0 %collective-permute-start.19 = (bf16[128,1024]{1,0:T(8,128)(2,1)}, bf16[128,1024]{1,0:T(8,128)(2,1)}, u32[]{:S(2)}, u32[]{:S(2)}) collective-permute-start(bf16[128,1024]{1,0:T(8,128)(2,1)} %get-tuple-element.169), channel_id=1, source_target_pairs={{0,6},{1,7},{2,0},{3,1},{4,2},{5,3},{6,4},{7,5},{8,14},{9,15},{10,... | collective-permute-start | bytes 786440 | tf_op jit(solution)/shard_map/ppermute | solution.py:425
  968.1 17.0 %collective-permute-start.20 = (bf16[128,2048]{1,0:T(8,128)(2,1)}, bf16[128,2048]{1,0:T(8,128)(2,1)}, u32[]{:S(2)}, u32[]{:S(2)}) collective-permute-start(bf16[128,2048]{1,0:T(8,128)(2,1)} %get-tuple-element.163), channel_id=1, source_target_pairs={{0,2},{1,3},{2,4},{3,5},{4,6},{5,7},{6,0},{7,1},{8,10},{9,11},{10,... | collective-permute-start | bytes 1572872 | tf_op jit(solution)/shard_map/ppermute | solution.py:424
  968.3 16.9 %collective-permute-start.21 = (bf16[128,2048]{1,0:T(8,128)(2,1)}, bf16[128,2048]{1,0:T(8,128)(2,1)}, u32[]{:S(2)}, u32[]{:S(2)}) collective-permute-start(bf16[128,2048]{1,0:T(8,128)(2,1)} %get-tuple-element.174), channel_id=1, source_target_pairs={{0,6},{1,7},{2,0},{3,1},{4,2},{5,3},{6,4},{7,5},{8,14},{9,15},{10,... | collective-permute-start | bytes 1572872 | tf_op jit(solution)/shard_map/ppermute | solution.py:425
  977.9 16.5 %collective-permute-start.22 = (bf16[128,2048]{1,0:T(8,128)(2,1)}, bf16[128,2048]{1,0:T(8,128)(2,1)}, u32[]{:S(2)}, u32[]{:S(2)}) collective-permute-start(bf16[128,2048]{1,0:T(8,128)(2,1)} %get-tuple-element.172), channel_id=1, source_target_pairs={{0,2},{1,3},{2,4},{3,5},{4,6},{5,7},{6,0},{7,1},{8,10},{9,11},{10,... | collective-permute-start | bytes 1572872 | tf_op jit(solution)/shard_map/ppermute | solution.py:424
  977.9 16.5 %collective-permute-start.23 = (bf16[128,2048]{1,0:T(8,128)(2,1)}, bf16[128,2048]{1,0:T(8,128)(2,1)}, u32[]{:S(2)}, u32[]{:S(2)}) collective-permute-start(bf16[128,2048]{1,0:T(8,128)(2,1)} %get-tuple-element.177), channel_id=1, source_target_pairs={{0,6},{1,7},{2,0},{3,1},{4,2},{5,3},{6,4},{7,5},{8,14},{9,15},{10,... | collective-permute-start | bytes 1572872 | tf_op jit(solution)/shard_map/ppermute | solution.py:425
Sparse Core Ops, SparseCore 0:
  9.8 48.5 all-gather.9
  60.0 45.7 all-gather.7
  107.4 80.9 all-gather.5
  189.8 81.3 all-gather.11

commit v3 on v2

--- a/solution.py
+++ b/solution.py
@@ -33,17 +33,25 @@
     return (vals * cos + swapped * sin).astype(BF16)
 
 
-def norm_rows(x_buf, out_buf, mean, rstd, gain, bias, start, count, width):
+def norm_rows(x_buf, out_buf, mean, rstd, gain, bias, start, count, col0, cols):
     at = pl.ds(start, count)
-    for c in range(width // LANES):
-        cols = pl.ds(c * LANES, LANES)
-        n = (x_buf[at, cols].astype(F32) - mean) * rstd
-        out_buf[at, cols] = (n * gain[:, cols] + bias[:, cols]).astype(BF16)
+    for c in range(col0, col0 + cols, LANES):
+        lanes = pl.ds(c, LANES)
+        n = (x_buf[at, lanes].astype(F32) - mean) * rstd
+        out_buf[at, lanes] = (n * gain[:, lanes] + bias[:, lanes]).astype(BF16)
+
+
+def dot_beside(acc, lhs, rhs, width, pieces, beside):
+    depth = width // pieces
+    for k in range(pieces):
+        beside(k * depth, depth)
+        part = jnp.dot(lhs[:, pl.ds(k * depth, depth)], rhs[pl.ds(k * depth, depth), :], preferred_element_type=F32)
+        acc[...] = part if k == 0 else acc[...] + part
 
 
 def expand_kernel(devs, width, q_tiles, up_tiles, aliased, x_hbm, mean_ref, rstd_ref, a_gain, a_bias, m_gain, m_bias, wq, wkv, wu, qc, qs, kc, ks, *refs):
     refs = refs[3:] if aliased else refs
-    q_out, kv_out, act_out, x_buf, a_buf, m_buf, pend, stat, sems = refs
+    q_out, kv_out, act_out, x_buf, a_buf, m_buf, pend, q_acc, stat, sems = refs
     m, n = pl.program_id(0), pl.program_id(1)
     rows = devs * ROWS
 
@@ -71,7 +79,7 @@
             fetch(0, d).wait()
             start = pl.multiple_of(d * ROWS, ROWS)
             mean, rstd = row_stats(start, ROWS)
-            norm_rows(x_buf, a_buf, mean, rstd, a_gain, a_bias, start, ROWS, width)
+            norm_rows(x_buf, a_buf, mean, rstd, a_gain, a_bias, start, ROWS, 0, width)
             return carry
 
         lax.fori_loop(0, devs, one, 0)
@@ -93,8 +101,9 @@
         count = rows // q_tiles
         start = pl.multiple_of(n * count, count)
         mean, rstd = row_stats(start, count)
-        norm_rows(x_buf, m_buf, mean, rstd, m_gain, m_bias, start, count, width)
-        acc = jnp.dot(a_buf[...], wq[...], preferred_element_type=F32)
+        dot_beside(q_acc, a_buf, wq, width, 16, lambda col0, cols: norm_rows(
+            x_buf, m_buf, mean, rstd, m_gain, m_bias, start, count, col0, cols))
+        acc = q_acc[...]
         cos, sin = qc[...].reshape(rows, LANES), qs[...].reshape(rows, LANES)
         for c in range(acc.shape[1] // LANES):
             part = rotate(acc[:, c * LANES:(c + 1) * LANES], cos, sin, first_half)
@@ -123,9 +132,9 @@
         count = pl.cdiv(pl.cdiv(rows, up_tiles - 1), 16) * 16
         start = pl.multiple_of(jnp.minimum((n - q_tiles - 2) * count, rows - count), 16)
         mean, rstd = row_stats(start, count)
-        norm_rows(x_buf, a_buf, mean, rstd, a_gain, a_bias, start, count, width)
         gelu_out()
-        up_dot()
+        dot_beside(pend, m_buf, wu, width, 8, lambda col0, cols: norm_rows(
+            x_buf, a_buf, mean, rstd, a_gain, a_bias, start, count, col0, cols))
 
     @pl.when(n == q_tiles + up_tiles + 1)
     def _():
@@ -177,7 +186,7 @@
         out_shape=out_shape,
         scratch_shapes=[
             pltpu.VMEM((rows, width), BF16), pltpu.VMEM((rows, width), BF16), pltpu.VMEM((rows, width), BF16),
-            pltpu.VMEM((rows, tu), F32), pltpu.VMEM((2, rows, LANES), F32), pltpu.SemaphoreType.DMA((devs,)),
+            pltpu.VMEM((rows, tu), F32), pltpu.VMEM((rows, tq), F32), pltpu.VMEM((2, rows, LANES), F32), pltpu.SemaphoreType.DMA((devs,)),
         ],
         input_output_aliases=aliases,
         compiler_params=pltpu.CompilerParams(vmem_limit_bytes=VMEM_LIMIT),
@@ -324,7 +333,7 @@
 
 def merge(up_lo, down_hi, below, above, up, down):
     blk, half = up_lo.shape
-    cw = min(1024, half)
+    cw = min(2048, half)
     any_spec = pl.BlockSpec(memory_space=pl.ANY)
     part = pl.BlockSpec((blk, cw), lambda j: (0, j))
     return pl.pallas_call(
@@ -348,7 +357,7 @@
 
 def finish(hidden, batch_id, col0, own, below, above, result):
     blk, cols = own.shape
-    cw = min(1024, cols)
+    cw = min(2048, cols)
     j0 = col0 // cw
     part = pl.BlockSpec((blk, cw), lambda j: (0, j))
     wide = pl.BlockSpec((None, blk, cw), lambda j: (batch_id, 0, j0 + j))

time: 1010 us -> 980 us (0.970)
  Pallas kernels: 874 us -> 844 us
    pallas_call x4, Pallas kernels: 417 us -> 391 us  [expand(): pl.pallas_call(functools.partial(expand_kernel, devs, width, q_tiles, up_...]
  transfers between devices with their start and end apart: 28 -> 28, of which waited for: 5 -> 4; matrix products, arithmetic and copies ran while one was open for 2% -> 2% of each run, Pallas kernels for 78% -> 78%
where the time goes in v3:
time: 980 us; the launch traced here: 974 us
  Pallas kernels  844 us (86%)
  waiting for transfers between devices  37.4 us (4%)
  starting transfers between devices  33 us (3%)
  blocking collectives  20.5 us (2%)
  other arithmetic  14.2 us (1%)
  between operations  14 us (1%)
  local copies, waits for them, and re-layouts  10.6 us (1%)
    pallas_call x4, Pallas kernels, expand(): pl.pallas_call(functools.partial(expand_kernel, devs, width, q_tiles, up_...  391 us
    pallas_call x9, Pallas kernels, contract(): pl.pallas_call(functools.partial(contract_kernel, num, None if add is Non...  335 us
    pallas_call x3, Pallas kernels, attend(): pl.pallas_call(functools.partial(attend_kernel, seq, head_dim), grid=(q_c...  81.9 us
    ppermute x10, starting transfers between devices, layer(): ring_down = lambda v: lax.ppermute(v, 'tp', down_ring)  30.9 us
    ppermute x10, waiting for transfers between devices, layer(): ring_up = lambda v: lax.ppermute(v, 'tp', up_ring)  28 us
    pallas_call x5, Pallas kernels, finish(): pl.pallas_call(finish_kernel, grid=(cols // cw,), in_specs=in_specs, out_...  20.7 us
    all_gather x1, blocking collectives, layer(): lax.all_gather(jnp.stack([mean[..., 0], rstd[..., 0]]), 'tp', axis=2, til...  20.5 us
  transfers between devices with their start and end apart: 28, of which 4 were waited for; matrix products, arithmetic and copies ran while one was open for 2% of the time, Pallas kernels for 78%

profile of v3, /device:TPU:112, one launch (start us, length us, event | category | flops | bytes accessed | tf_op | source)
XLA Modules:
  0.0 974.0 jit_solution(15865887229219534736)
XLA Ops:
  6.6 3.1 fusion.7
  9.8 0.7 all-gather.8.cloned.1.call-update
  10.6 4.6 fusion.6
  15.3 0.1 all-gather.12.cloned.1.call-start
  15.3 0.6 all-gather.12.cloned.1.call-update
  16.0 4.3 convert_reduce_fusion
  20.3 4.7 fusion.1
  25.0 20.5 %all-gather = f32[2,3,1024]{2,0,1:T(2,128)S(1)} all-gather(f32[2,3,128]{2,0,1:T(2,128)S(1)} %pad_maximum_fusion.4), channel_id=2, replica_groups=mesh['dp'=2,'tp'=8] {'tp'}, dimensions={2}, use_global_device_ids=true | all-gather | bytes 27648 | tf_op jit(solution)/shard_map/all_gather | solution.py:417
  45.6 0.1 pad.5.clone
  45.7 0.1 pad.2.clone
  45.7 1.9 fusion.4
  47.7 0.7 broadcast_add_fusion
  48.3 2.2 fusion.2
  50.5 7.9 all-gather.10.cloned.1.call-done.x_hbm
  58.4 2.7 broadcast_in_dim.6.mean_ref.rstd_ref
  61.0 67.9 %expand.4 = (bf16[8,128,1024]{2,1,0:T(8,128)(2,1)}, bf16[8,128,128]{2,1,0:T(8,128)(2,1)}, bf16[8,128,4096]{2,1,0:T(8,128)(2,1)}) custom-call(bf16[8,64,8192]{2,1,0:T(8,128)(2,1)} %all-gather.10.cloned.1.call-done.x_hbm, f32[2,3,8,128,128]{4,3,2,1,0:T(8,128)} %broadcast_in_dim.6.mean_ref.rstd_ref, f32[2,3,8,128,128]{4,3,2,1,0:T(8,128)} %broadcast_in_dim.6.mean_ref.rstd_ref, ...), custom_call_target="tpu_custom_call" | custom-call | flops 44023414784 | bytes 83886080 | tf_op jit(solution)/shard_map/expand/pallas_call | solution.py:181
  129.0 67.3 %expand.5 = (bf16[8,128,1024]{2,1,0:T(8,128)(2,1)}, bf16[8,128,128]{2,1,0:T(8,128)(2,1)}, bf16[8,128,4096]{2,1,0:T(8,128)(2,1)}) custom-call(bf16[8,64,8192]{2,1,0:T(8,128)(2,1)} %all-gather.8.cloned.1.call-done.x_hbm, f32[2,3,8,128,128]{4,3,2,1,0:T(8,128)} %broadcast_in_dim.6.mean_ref.rstd_ref, ...), custom_call_target="tpu_custom_call", output_to_operand_aliasing={{0}: (14, {}), {1}: (15, {}), {2}: (16, {})} | custom-call | flops 44023414784 | bytes 83886080 | tf_op jit(solution)/shard_map/expand/pallas_call | solution.py:181
  196.2 27.2 %attend.3 = bf16[1024,1024]{1,0:T(8,128)(2,1)} custom-call(bf16[1024,1024]{1,0:T(8,128)(2,1)} %bitcast.59, bf16[1024,128]{1,0:T(8,128)(2,1)} %bitcast.62), custom_call_target="tpu_custom_call" | custom-call | flops 8589934592 | bytes 4194304 | tf_op jit(solution)/shard_map/attend/pallas_call | solution.py:234
  223.5 52.4 %contract_pair.4 = bf16[4,128,8192]{2,1,0:T(8,128)(2,1)} custom-call(s32[4]{0:T(128)} %get-tuple-element.135.order, bf16[8,128,1024]{2,1,0:T(8,128)(2,1)} %bitcast.56, bf16[8,128,4096]{2,1,0:T(8,128)(2,1)} %get-tuple-element.101.act_hbm, bf16[1024,8192]{1,0:T(8,128)(2,1)} %wo_hbm.17, bf16[4096,8192]{1,0:T(8,128)(2,1)} %wd_hbm.17), custom_call_target="tpu_custom_call" | custom-call | flops 42949672960 | bytes 83886080 | tf_op jit(solution)/shard_map/contract_pair/pallas_call | solution.py:314
  275.9 0.6 collective-permute-start
  276.5 0.5 broadcast_add_fusion.1.order
  277.0 128.2 %expand.6 = (bf16[8,128,1024]{2,1,0:T(8,128)(2,1)}, bf16[8,128,128]{2,1,0:T(8,128)(2,1)}, bf16[8,128,4096]{2,1,0:T(8,128)(2,1)}) custom-call(bf16[8,128,8192]{2,1,0:T(8,128)(2,1)} %all-gather.6.cloned.1.call-done.x_hbm, f32[2,3,8,128,128]{4,3,2,1,0:T(8,128)} %broadcast_in_dim.6.mean_ref.rstd_ref, f32[2,3,8,128,128]{4,3,2,1,0:T(8,128)} %broadcast_in_dim.6.mean_ref.rstd_ref, ...), custom_call_target="tpu_custom_call" | custom-call | flops 88046829568 | bytes 83886080 | tf_op jit(solution)/shard_map/expand/pallas_call | solution.py:181
  405.2 53.8 %contract_own.5 = (bf16[128,4096]{1,0:T(8,128)(2,1)}, bf16[128,4096]{1,0:T(8,128)(2,1)}, bf16[128,8192]{1,0:T(8,128)(2,1)}, bf16[128,8192]{1,0:T(8,128)(2,1)}, f...) custom-call(s32[4]{0:T(128)} %broadcast_add_fusion.1.order, bf16[8,128,1024]{2,1,0:T(8,128)(2,1)} %bitcast.57, ...), custom_call_target="tpu_custom_call" | custom-call | flops 42949672960 | bytes 83886080 | tf_op jit(solution)/shard_map/contract_own/pallas_call | solution.py:314
  459.0 0.3 collective-permute-start.1
  459.3 27.3 %attend.4 = bf16[1024,1024]{1,0:T(8,128)(2,1)} custom-call(bf16[1024,1024]{1,0:T(8,128)(2,1)} %bitcast.58, bf16[1024,128]{1,0:T(8,128)(2,1)} %bitcast.61), custom_call_target="tpu_custom_call" | custom-call | flops 8589934592 | bytes 4194304 | tf_op jit(solution)/shard_map/attend/pallas_call | solution.py:234
  486.6 3.0 collective-permute-start.2
  489.6 52.1 %contract_pair.5 = bf16[4,128,8192]{2,1,0:T(8,128)(2,1)} custom-call(s32[4]{0:T(128)} %get-tuple-element.135.order, bf16[8,128,1024]{2,1,0:T(8,128)(2,1)} %bitcast.53, bf16[8,128,4096]{2,1,0:T(8,128)(2,1)} %get-tuple-element.111.act_hbm, bf16[1024,8192]{1,0:T(8,128)(2,1)} %wo_hbm.17, bf16[4096,8192]{1,0:T(8,128)(2,1)} %wd_hbm.17), custom_call_target="tpu_custom_call" | custom-call | flops 42949672960 | bytes 83886080 | tf_op jit(solution)/shard_map/contract_pair/pallas_call | solution.py:314
  541.7 0.1 collective-permute-start.5
  541.8 3.9 merge.5
  545.7 3.2 collective-permute-start.4
  549.0 127.7 %expand.7 = (bf16[8,128,1024]{2,1,0:T(8,128)(2,1)}, bf16[8,128,128]{2,1,0:T(8,128)(2,1)}, bf16[8,128,4096]{2,1,0:T(8,128)(2,1)}) custom-call(bf16[8,128,8192]{2,1,0:T(8,128)(2,1)} %all-gather.12.cloned.1.call-done.x_hbm, f32[2,3,8,128,128]{4,3,2,1,0:T(8,128)} %broadcast_in_dim.6.mean_ref.rstd_ref, f32[2,3,8,128,128]{4,3,2,1,0:T(8,128)} %broadcast_in_dim.6.mean_ref.rstd_ref, ...), custom_call_target="tpu_custom_call" | custom-call | flops 88046829568 | bytes 83886080 | tf_op jit(solution)/shard_map/expand/pallas_call | solution.py:181
  676.7 5.9 finish.5.refs_0_
  682.6 53.8 %contract_own.6 = (bf16[128,4096]{1,0:T(8,128)(2,1)}, bf16[128,4096]{1,0:T(8,128)(2,1)}, bf16[128,8192]{1,0:T(8,128)(2,1)}, bf16[128,8192]{1,0:T(8,128)(2,1)}, f...) custom-call(s32[4]{0:T(128)} %broadcast_add_fusion.1.order, bf16[8,128,1024]{2,1,0:T(8,128)(2,1)} %bitcast.54, ...), custom_call_target="tpu_custom_call" | custom-call | flops 42949672960 | bytes 83886080 | tf_op jit(solution)/shard_map/contract_own/pallas_call | solution.py:314
  736.4 0.1 collective-permute-start.6
  736.5 3.2 collective-permute-start.7
  739.7 27.4 %attend.5 = bf16[1024,1024]{1,0:T(8,128)(2,1)} custom-call(bf16[1024,1024]{1,0:T(8,128)(2,1)} %bitcast.55, bf16[1024,128]{1,0:T(8,128)(2,1)} %bitcast.60), custom_call_target="tpu_custom_call" | custom-call | flops 8589934592 | bytes 4194304 | tf_op jit(solution)/shard_map/attend/pallas_call | solution.py:234
  767.1 3.9 merge.6
  771.1 28.8 %contract_pair.6 = bf16[4,128,4096]{2,1,0:T(8,128)(2,1)} custom-call(s32[4]{0:T(128)} %get-tuple-element.135.order, bf16[8,128,1024]{2,1,0:T(8,128)(2,1)} %bitcast.24, bf16[8,128,4096]{2,1,0:T(8,128)(2,1)} %get-tuple-element.134.act_hbm, bf16[1024,8192]{1,0:T(8,128)(2,1)} %wo_hbm.17, bf16[4096,8192]{1,0:T(8,128)(2,1)} %wd_hbm.17), custom_call_target="tpu_custom_call" | custom-call | flops 21474836480 | bytes 41943040 | tf_op jit(solution)/shard_map/contract_pair/pallas_call | solution.py:314
  799.9 0.1 collective-permute-start.8
  800.0 28.8 %contract_pair.7 = bf16[4,128,4096]{2,1,0:T(8,128)(2,1)} custom-call(s32[4]{0:T(128)} %get-tuple-element.135.order, bf16[8,128,1024]{2,1,0:T(8,128)(2,1)} %bitcast.25, bf16[8,128,4096]{2,1,0:T(8,128)(2,1)} %get-tuple-element.134.act_hbm, bf16[1024,8192]{1,0:T(8,128)(2,1)} %wo_hbm.17, bf16[4096,8192]{1,0:T(8,128)(2,1)} %wd_hbm.17), custom_call_target="tpu_custom_call" | custom-call | flops 21474836480 | bytes 41943040 | tf_op jit(solution)/shard_map/contract_pair/pallas_call | solution.py:314
  828.8 0.5 collective-permute-start.11
  829.4 3.2 collective-permute-start.10
  832.6 29.9 %contract_own.7 = (bf16[128,2048]{1,0:T(8,128)(2,1)}, bf16[128,2048]{1,0:T(8,128)(2,1)}, bf16[128,4096]{1,0:T(8,128)(2,1)}, bf16[128,4096]{1,0:T(8,128)(2,1)}, f...) custom-call(s32[4]{0:T(128)} %broadcast_add_fusion.1.order, bf16[8,128,1024]{2,1,0:T(8,128)(2,1)} %bitcast.26, ...), custom_call_target="tpu_custom_call" | custom-call | flops 21474836480 | bytes 41943040 | tf_op jit(solution)/shard_map/contract_own/pallas_call | solution.py:314
  862.5 0.1 collective-permute-start.12
  862.6 16.8 %collective-permute-done.9.below = bf16[128,8192]{1,0:T(8,128)(2,1)} collective-permute-done((bf16[128,8192]{1,0:T(8,128)(2,1)}, bf16[128,8192]{1,0:T(8,128)(2,1)}, u32[]{:S(2)}, u32[]{:S(2)}) %collective-permute-start.9) | collective-permute-done | bytes 2097184 | tf_op jit(solution)/shard_map/ppermute | solution.py:433
  879.4 5.9 finish.6.refs_0_
  885.3 2.1 collective-permute-start.13
  887.4 17.9 %contract_own.8 = (bf16[128,1024]{1,0:T(8,128)(2,1)}, bf16[128,1024]{1,0:T(8,128)(2,1)}, bf16[128,2048]{1,0:T(8,128)(2,1)}, bf16[128,2048]{1,0:T(8,128)(2,1)}, f...) custom-call(s32[4]{0:T(128)} %broadcast_add_fusion.1.order, bf16[8,128,1024]{2,1,0:T(8,128)(2,1)} %bitcast.27, ...), custom_call_target="tpu_custom_call" | custom-call | flops 10737418240 | bytes 20971520 | tf_op jit(solution)/shard_map/contract_own/pallas_call | solution.py:314
  905.3 0.1 collective-permute-start.14
  905.4 3.2 collective-permute-start.15
  908.6 2.9 merge.7
  911.6 3.2 collective-permute-start.17
  914.8 17.9 %contract_own.9 = (bf16[128,1024]{1,0:T(8,128)(2,1)}, bf16[128,1024]{1,0:T(8,128)(2,1)}, bf16[128,2048]{1,0:T(8,128)(2,1)}, bf16[128,2048]{1,0:T(8,128)(2,1)}, f...) custom-call(s32[4]{0:T(128)} %broadcast_add_fusion.1.order, bf16[8,128,1024]{2,1,0:T(8,128)(2,1)} %bitcast.28, ...), custom_call_target="tpu_custom_call" | custom-call | flops 10737418240 | bytes 20971520 | tf_op jit(solution)/shard_map/contract_own/pallas_call | solution.py:314
  932.7 0.1 collective-permute-start.18
  932.8 3.2 collective-permute-start.19
  936.0 2.2 merge.8
  938.3 3.2 collective-permute-start.21
  941.5 3.5 finish.7.refs_0_
  945.0 2.2 merge.9
  947.3 3.2 collective-permute-start.23
  950.5 4.4 collective-permute-done.20.below
  954.9 2.7 finish.8.refs_0_
  957.6 6.7 collective-permute-done.22.below
  964.4 2.7 finish.9
  (47 shorter events, 0.4 us)
Async XLA Ops:
  6.5 51.8 %all-gather.10.cloned.1.call-start = ((), (), s32[]{:S(2)}) async-start(), calls=%async_computation.2 | async-start | bytes 9437184 | tf_op jit(solution)/shard_map/all_gather | solution.py:403
  9.7 119.3 %all-gather.8.cloned.1.call-start = ((), (), s32[]{:S(2)}) async-start(), calls=%async_computation.1 | async-start | bytes 9437184 | tf_op jit(solution)/shard_map/all_gather | solution.py:403
  10.5 266.5 %all-gather.6.cloned.1.call-start = ((), (), s32[]{:S(2)}) async-start(), calls=%async_computation | async-start | bytes 18874368 | tf_op jit(solution)/shard_map/all_gather | solution.py:403
  15.3 530.5 %all-gather.12.cloned.1.call-start = ((), (), s32[]{:S(2)}) async-start(), calls=%async_computation.3 | async-start | bytes 18874368 | tf_op jit(solution)/shard_map/all_gather | solution.py:403
  20.3 25.3 %copy-start = (s32[1024]{0:T(1024)S(1)}, s32[1024]{0:T(1024)}, u32[]{:S(2)}) copy-start(s32[1024]{0:T(1024)} %param.19) | copy-start | bytes 12292
  275.9 129.2 %collective-permute-start = (bf16[4,128,8192]{2,1,0:T(8,128)(2,1)}, bf16[4,128,8192]{2,1,0:T(8,128)(2,1)}, u32[]{:S(2)}, u32[]{:S(2)}) collective-permute-start(bf16[4,128,8192]{2,1,0:T(8,128)(2,1)} %contract_pair.4), channel_id=1, source_target_pairs={{0,1},{1,0},{2,3},{3,2},{4,5},{5,4},{6,7},{7,6},{8,9},{9,8},{10,11... | collective-permute-start | bytes 25165832 | tf_op jit(solution)/shard_map/ppermute | solution.py:449
  459.0 82.8 %collective-permute-start.1 = (bf16[128,4096]{1,0:T(8,128)(2,1)}, bf16[128,4096]{1,0:T(8,128)(2,1)}, u32[]{:S(2)}, u32[]{:S(2)}) collective-permute-start(bf16[128,4096]{1,0:T(8,128)(2,1)} %get-tuple-element.108), channel_id=1, source_target_pairs={{0,2},{1,3},{2,4},{3,5},{4,6},{5,7},{6,0},{7,1},{8,10},{9,11},{10,... | collective-permute-start | bytes 3145736 | tf_op jit(solution)/shard_map/ppermute | solution.py:433
  486.6 55.2 %collective-permute-start.2 = (bf16[128,4096]{1,0:T(8,128)(2,1)}, bf16[128,4096]{1,0:T(8,128)(2,1)}, u32[]{:S(2)}, u32[]{:S(2)}) collective-permute-start(bf16[128,4096]{1,0:T(8,128)(2,1)} %get-tuple-element.114), channel_id=1, source_target_pairs={{0,6},{1,7},{2,0},{3,1},{4,2},{5,3},{6,4},{7,5},{8,14},{9,15},{10,... | collective-permute-start | bytes 3145736 | tf_op jit(solution)/shard_map/ppermute | solution.py:434
  541.7 140.9 %collective-permute-start.5 = (bf16[4,128,8192]{2,1,0:T(8,128)(2,1)}, bf16[4,128,8192]{2,1,0:T(8,128)(2,1)}, u32[]{:S(2)}, u32[]{:S(2)}) collective-permute-start(bf16[4,128,8192]{2,1,0:T(8,128)(2,1)} %contract_pair.5), channel_id=1, source_target_pairs={{0,1},{1,0},{2,3},{3,2},{4,5},{5,4},{6,7},{7,6},{8,9},{9,8},{10,11... | collective-permute-start | bytes 25165832 | tf_op jit(solution)/shard_map/ppermute | solution.py:449
  545.7 131.0 %collective-permute-start.3 = (bf16[128,8192]{1,0:T(8,128)(2,1)}, bf16[128,8192]{1,0:T(8,128)(2,1)}, u32[]{:S(2)}, u32[]{:S(2)}) collective-permute-start(bf16[128,8192]{1,0:T(8,128)(2,1)} %get-tuple-element.117), channel_id=1, source_target_pairs={{0,2},{1,3},{2,4},{3,5},{4,6},{5,7},{6,0},{7,1},{8,10},{9,11},{10,... | collective-permute-start | bytes 6291464 | tf_op jit(solution)/shard_map/ppermute | solution.py:433
  545.7 130.9 %collective-permute-start.4 = (bf16[128,8192]{1,0:T(8,128)(2,1)}, bf16[128,8192]{1,0:T(8,128)(2,1)}, u32[]{:S(2)}, u32[]{:S(2)}) collective-permute-start(bf16[128,8192]{1,0:T(8,128)(2,1)} %get-tuple-element.121), channel_id=1, source_target_pairs={{0,6},{1,7},{2,0},{3,1},{4,2},{5,3},{6,4},{7,5},{8,14},{9,15},{10,... | collective-permute-start | bytes 6291464 | tf_op jit(solution)/shard_map/ppermute | solution.py:434
  736.4 30.7 %collective-permute-start.6 = (bf16[128,4096]{1,0:T(8,128)(2,1)}, bf16[128,4096]{1,0:T(8,128)(2,1)}, u32[]{:S(2)}, u32[]{:S(2)}) collective-permute-start(bf16[128,4096]{1,0:T(8,128)(2,1)} %get-tuple-element.125), channel_id=1, source_target_pairs={{0,2},{1,3},{2,4},{3,5},{4,6},{5,7},{6,0},{7,1},{8,10},{9,11},{10,... | collective-permute-start | bytes 3145736 | tf_op jit(solution)/shard_map/ppermute | solution.py:433
  736.5 30.6 %collective-permute-start.7 = (bf16[128,4096]{1,0:T(8,128)(2,1)}, bf16[128,4096]{1,0:T(8,128)(2,1)}, u32[]{:S(2)}, u32[]{:S(2)}) collective-permute-start(bf16[128,4096]{1,0:T(8,128)(2,1)} %get-tuple-element.129), channel_id=1, source_target_pairs={{0,6},{1,7},{2,0},{3,1},{4,2},{5,3},{6,4},{7,5},{8,14},{9,15},{10,... | collective-permute-start | bytes 3145736 | tf_op jit(solution)/shard_map/ppermute | solution.py:434
  799.9 32.7 %collective-permute-start.8 = (bf16[4,128,4096]{2,1,0:T(8,128)(2,1)}, bf16[4,128,4096]{2,1,0:T(8,128)(2,1)}, u32[]{:S(2)}, u32[]{:S(2)}) collective-permute-start(bf16[4,128,4096]{2,1,0:T(8,128)(2,1)} %contract_pair.6), channel_id=1, source_target_pairs={{0,1},{1,0},{2,3},{3,2},{4,5},{5,4},{6,7},{7,6},{8,9},{9,8},{10,11... | collective-permute-start | bytes 12582920 | tf_op jit(solution)/shard_map/ppermute | solution.py:449
  828.8 58.6 %collective-permute-start.11 = (bf16[4,128,4096]{2,1,0:T(8,128)(2,1)}, bf16[4,128,4096]{2,1,0:T(8,128)(2,1)}, u32[]{:S(2)}, u32[]{:S(2)}) collective-permute-start(bf16[4,128,4096]{2,1,0:T(8,128)(2,1)} %contract_pair.7), channel_id=1, source_target_pairs={{0,1},{1,0},{2,3},{3,2},{4,5},{5,4},{6,7},{7,6},{8,9},{9,8},{10,11... | collective-permute-start | bytes 12582920 | tf_op jit(solution)/shard_map/ppermute | solution.py:449
  829.4 50.0 %collective-permute-start.9 = (bf16[128,8192]{1,0:T(8,128)(2,1)}, bf16[128,8192]{1,0:T(8,128)(2,1)}, u32[]{:S(2)}, u32[]{:S(2)}) collective-permute-start(bf16[128,8192]{1,0:T(8,128)(2,1)} %get-tuple-element.132), channel_id=1, source_target_pairs={{0,2},{1,3},{2,4},{3,5},{4,6},{5,7},{6,0},{7,1},{8,10},{9,11},{10,... | collective-permute-start | bytes 6291464 | tf_op jit(solution)/shard_map/ppermute | solution.py:433
  829.4 50.0 %collective-permute-start.10 = (bf16[128,8192]{1,0:T(8,128)(2,1)}, bf16[128,8192]{1,0:T(8,128)(2,1)}, u32[]{:S(2)}, u32[]{:S(2)}) collective-permute-start(bf16[128,8192]{1,0:T(8,128)(2,1)} %get-tuple-element.141), channel_id=1, source_target_pairs={{0,6},{1,7},{2,0},{3,1},{4,2},{5,3},{6,4},{7,5},{8,14},{9,15},{10,... | collective-permute-start | bytes 6291464 | tf_op jit(solution)/shard_map/ppermute | solution.py:434
  862.5 46.1 %collective-permute-start.12 = (bf16[128,2048]{1,0:T(8,128)(2,1)}, bf16[128,2048]{1,0:T(8,128)(2,1)}, u32[]{:S(2)}, u32[]{:S(2)}) collective-permute-start(bf16[128,2048]{1,0:T(8,128)(2,1)} %get-tuple-element.139), channel_id=1, source_target_pairs={{0,2},{1,3},{2,4},{3,5},{4,6},{5,7},{6,0},{7,1},{8,10},{9,11},{10,... | collective-permute-start | bytes 1572872 | tf_op jit(solution)/shard_map/ppermute | solution.py:433
  885.3 23.3 %collective-permute-start.13 = (bf16[128,2048]{1,0:T(8,128)(2,1)}, bf16[128,2048]{1,0:T(8,128)(2,1)}, u32[]{:S(2)}, u32[]{:S(2)}) collective-permute-start(bf16[128,2048]{1,0:T(8,128)(2,1)} %get-tuple-element.147), channel_id=1, source_target_pairs={{0,6},{1,7},{2,0},{3,1},{4,2},{5,3},{6,4},{7,5},{8,14},{9,15},{10,... | collective-permute-start | bytes 1572872 | tf_op jit(solution)/shard_map/ppermute | solution.py:434
  905.3 27.5 %collective-permute-start.14 = (bf16[128,1024]{1,0:T(8,128)(2,1)}, bf16[128,1024]{1,0:T(8,128)(2,1)}, u32[]{:S(2)}, u32[]{:S(2)}) collective-permute-start(bf16[128,1024]{1,0:T(8,128)(2,1)} %get-tuple-element.144), channel_id=1, source_target_pairs={{0,2},{1,3},{2,4},{3,5},{4,6},{5,7},{6,0},{7,1},{8,10},{9,11},{10,... | collective-permute-start | bytes 786440 | tf_op jit(solution)/shard_map/ppermute | solution.py:433
  905.4 30.6 %collective-permute-start.15 = (bf16[128,1024]{1,0:T(8,128)(2,1)}, bf16[128,1024]{1,0:T(8,128)(2,1)}, u32[]{:S(2)}, u32[]{:S(2)}) collective-permute-start(bf16[128,1024]{1,0:T(8,128)(2,1)} %get-tuple-element.160), channel_id=1, source_target_pairs={{0,6},{1,7},{2,0},{3,1},{4,2},{5,3},{6,4},{7,5},{8,14},{9,15},{10,... | collective-permute-start | bytes 786440 | tf_op jit(solution)/shard_map/ppermute | solution.py:434
  911.6 26.7 %collective-permute-start.16 = (bf16[128,4096]{1,0:T(8,128)(2,1)}, bf16[128,4096]{1,0:T(8,128)(2,1)}, u32[]{:S(2)}, u32[]{:S(2)}) collective-permute-start(bf16[128,4096]{1,0:T(8,128)(2,1)} %get-tuple-element.150), channel_id=1, source_target_pairs={{0,2},{1,3},{2,4},{3,5},{4,6},{5,7},{6,0},{7,1},{8,10},{9,11},{10,... | collective-permute-start | bytes 3145736 | tf_op jit(solution)/shard_map/ppermute | solution.py:433
  911.6 30.0 %collective-permute-start.17 = (bf16[128,4096]{1,0:T(8,128)(2,1)}, bf16[128,4096]{1,0:T(8,128)(2,1)}, u32[]{:S(2)}, u32[]{:S(2)}) collective-permute-start(bf16[128,4096]{1,0:T(8,128)(2,1)} %get-tuple-element.165), channel_id=1, source_target_pairs={{0,6},{1,7},{2,0},{3,1},{4,2},{5,3},{6,4},{7,5},{8,14},{9,15},{10,... | collective-permute-start | bytes 3145736 | tf_op jit(solution)/shard_map/ppermute | solution.py:434
  932.7 12.3 %collective-permute-start.18 = (bf16[128,1024]{1,0:T(8,128)(2,1)}, bf16[128,1024]{1,0:T(8,128)(2,1)}, u32[]{:S(2)}, u32[]{:S(2)}) collective-permute-start(bf16[128,1024]{1,0:T(8,128)(2,1)} %get-tuple-element.157), channel_id=1, source_target_pairs={{0,2},{1,3},{2,4},{3,5},{4,6},{5,7},{6,0},{7,1},{8,10},{9,11},{10,... | collective-permute-start | bytes 786440 | tf_op jit(solution)/shard_map/ppermute | solution.py:433
  932.8 12.2 %collective-permute-start.19 = (bf16[128,1024]{1,0:T(8,128)(2,1)}, bf16[128,1024]{1,0:T(8,128)(2,1)}, u32[]{:S(2)}, u32[]{:S(2)}) collective-permute-start(bf16[128,1024]{1,0:T(8,128)(2,1)} %get-tuple-element.169), channel_id=1, source_target_pairs={{0,6},{1,7},{2,0},{3,1},{4,2},{5,3},{6,4},{7,5},{8,14},{9,15},{10,... | collective-permute-start | bytes 786440 | tf_op jit(solution)/shard_map/ppermute | solution.py:434
  938.3 16.6 %collective-permute-start.20 = (bf16[128,2048]{1,0:T(8,128)(2,1)}, bf16[128,2048]{1,0:T(8,128)(2,1)}, u32[]{:S(2)}, u32[]{:S(2)}) collective-permute-start(bf16[128,2048]{1,0:T(8,128)(2,1)} %get-tuple-element.163), channel_id=1, source_target_pairs={{0,2},{1,3},{2,4},{3,5},{4,6},{5,7},{6,0},{7,1},{8,10},{9,11},{10,... | collective-permute-start | bytes 1572872 | tf_op jit(solution)/shard_map/ppermute | solution.py:433
  938.3 16.6 %collective-permute-start.21 = (bf16[128,2048]{1,0:T(8,128)(2,1)}, bf16[128,2048]{1,0:T(8,128)(2,1)}, u32[]{:S(2)}, u32[]{:S(2)}) collective-permute-start(bf16[128,2048]{1,0:T(8,128)(2,1)} %get-tuple-element.174), channel_id=1, source_target_pairs={{0,6},{1,7},{2,0},{3,1},{4,2},{5,3},{6,4},{7,5},{8,14},{9,15},{10,... | collective-permute-start | bytes 1572872 | tf_op jit(solution)/shard_map/ppermute | solution.py:434
  947.3 17.1 %collective-permute-start.22 = (bf16[128,2048]{1,0:T(8,128)(2,1)}, bf16[128,2048]{1,0:T(8,128)(2,1)}, u32[]{:S(2)}, u32[]{:S(2)}) collective-permute-start(bf16[128,2048]{1,0:T(8,128)(2,1)} %get-tuple-element.172), channel_id=1, source_target_pairs={{0,2},{1,3},{2,4},{3,5},{4,6},{5,7},{6,0},{7,1},{8,10},{9,11},{10,... | collective-permute-start | bytes 1572872 | tf_op jit(solution)/shard_map/ppermute | solution.py:433
  947.3 17.1 %collective-permute-start.23 = (bf16[128,2048]{1,0:T(8,128)(2,1)}, bf16[128,2048]{1,0:T(8,128)(2,1)}, u32[]{:S(2)}, u32[]{:S(2)}) collective-permute-start(bf16[128,2048]{1,0:T(8,128)(2,1)} %get-tuple-element.177), channel_id=1, source_target_pairs={{0,6},{1,7},{2,0},{3,1},{4,2},{5,3},{6,4},{7,5},{8,14},{9,15},{10,... | collective-permute-start | bytes 1572872 | tf_op jit(solution)/shard_map/ppermute | solution.py:434
Sparse Core Ops, SparseCore 0:
  9.8 48.5 all-gather.9
  60.0 45.7 all-gather.7
  107.4 80.9 all-gather.5
  189.8 81.3 all-gather.11
